TPU v7x, 16 devices: a 4x2x1 block of a 4x4x8 slice. The times are simulated.
16 devices in a mesh: dp: 2 (over y, z), ep: 8 (over x, core).
Axes of the slice: x: 4, y: 2, z: 1, core: 2. Of those that a mesh axis runs over, the one named last changes fastest.
The devices are a block of a 4x4x8 slice.
Arguments:
- hidden: bfloat16 [2048, 5120], P(('dp', 'ep')), parts along dimension 0
- positions: int32 [2048], P(('dp', 'ep')), parts along dimension 0
- ckv_cache: bfloat16 [2048, 256, 512], P(('dp', 'ep')), parts along dimension 0
- kpe_cache: bfloat16 [2048, 256, 64], P(('dp', 'ep')), parts along dimension 0
- topk_ids: int32 [2048, 6], P(('dp', 'ep')), parts along dimension 0
- attn_gain: bfloat16 [5120], replicated
- w_dq: bfloat16 [5120, 1536], replicated
- q_gain: bfloat16 [1536], replicated
- w_uq: bfloat16 [1536, 3072], replicated
- w_dkv: bfloat16 [5120, 576], replicated
- kv_gain: bfloat16 [512], replicated
- w_uk: bfloat16 [512, 2048], replicated
- w_uv: bfloat16 [512, 2048], replicated
- w_out: bfloat16 [2048, 5120], replicated
- ffn_gain: bfloat16 [5120], replicated
- w_router: bfloat16 [5120, 16], replicated
- w_gate: bfloat16 [16, 5120, 1536], P('ep')
- w_up: bfloat16 [16, 5120, 1536], P('ep')
- w_down: bfloat16 [16, 1536, 5120], P('ep')
- shared_gate: bfloat16 [5120, 3072], replicated
- shared_up: bfloat16 [5120, 3072], replicated
- shared_down: bfloat16 [3072, 5120], replicated
Outputs:
- output 1: bfloat16 [2048, 5120], P(('dp', 'ep')), parts along dimension 0
- output 2: bfloat16 [2048, 512], P(('dp', 'ep')), parts along dimension 0
- output 3: bfloat16 [2048, 64], P(('dp', 'ep')), parts along dimension 0
There are 2 independent parts. A program takes and returns all parts, laid end to end along the dimension named above; an argument that names none is the same for every part.
All inputs are finite; a program needn't handle non-finite values.
Results may differ from a plain program's by a relative error of at most 0.0153546.
Values are sent between devices in bfloat16 or wider.
A program may use at most 768 MiB of HBM per device.

v0:
```python
import jax
import jax.numpy as jnp
from jax import lax
from jax.sharding import PartitionSpec as P

NOPE_DIM = 128
ROPE_DIM = 64
VALUE_DIM = 128
QK_DIM = NOPE_DIM + ROPE_DIM
EPSILON = 1e-6
ROUTE_SCALE = 2.5
ROPE_BASE = 10000.0
CAP_FACTOR = 2


def rms_norm(vec, gain):
    vec = vec.astype(jnp.float32)
    scale = lax.rsqrt(jnp.mean(vec * vec, axis=-1, keepdims=True) + EPSILON)
    return vec * scale * gain.astype(jnp.float32)


def rotary(vec, positions):
    half = ROPE_DIM // 2
    freqs = ROPE_BASE ** (-jnp.arange(half).astype(jnp.float32) / half)
    angle = positions.astype(jnp.float32)[..., None] * freqs
    cosine = jnp.cos(angle)
    sine = jnp.sin(angle)
    first = vec[..., :half]
    second = vec[..., half:]
    return jnp.concatenate([first * cosine - second * sine, first * sine + second * cosine], axis=-1)


def attention_block(hidden, positions, ckv_cache, kpe_cache, attn_gain, w_dq, q_gain, w_uq, w_dkv, kv_gain, w_uk, w_uv, w_out):
    tokens = hidden.shape[0]
    kv_rank = w_uk.shape[0]
    heads = w_uk.shape[1] // NOPE_DIM
    cache_len = ckv_cache.shape[1]
    normed = rms_norm(hidden, attn_gain).astype(jnp.bfloat16)
    c_q = rms_norm(jnp.dot(normed, w_dq, preferred_element_type=jnp.float32), q_gain).astype(jnp.bfloat16)
    query = jnp.dot(c_q, w_uq, preferred_element_type=jnp.float32).astype(jnp.bfloat16).reshape(tokens, heads, QK_DIM)
    q_nope = query[:, :, :NOPE_DIM]
    q_rot = rotary(query[:, :, NOPE_DIM:].astype(jnp.float32), positions[:, None]).astype(jnp.bfloat16)
    kv_proj = jnp.dot(normed, w_dkv, preferred_element_type=jnp.float32)
    c_new = rms_norm(kv_proj[:, :kv_rank], kv_gain).astype(jnp.bfloat16)
    k_new = rotary(kv_proj[:, kv_rank:], positions).astype(jnp.bfloat16)
    q_abs = jnp.einsum('thn,chn->thc', q_nope, w_uk.reshape(kv_rank, heads, NOPE_DIM), preferred_element_type=jnp.float32).astype(jnp.bfloat16)
    scale = QK_DIM ** -0.5
    s_cache = (jnp.einsum('thc,tsc->ths', q_abs, ckv_cache, preferred_element_type=jnp.float32) + jnp.einsum('thr,tsr->ths', q_rot, kpe_cache, preferred_element_type=jnp.float32)) * scale
    valid = jnp.arange(cache_len)[None, None, :] < positions[:, None, None]
    s_cache = jnp.where(valid, s_cache, -1e30)
    s_self = (jnp.einsum('thc,tc->th', q_abs, c_new, preferred_element_type=jnp.float32) + jnp.einsum('thr,tr->th', q_rot, k_new, preferred_element_type=jnp.float32)) * scale
    peak = jnp.maximum(jnp.max(s_cache, axis=2), s_self)
    e_cache = jnp.exp(s_cache - peak[:, :, None])
    e_self = jnp.exp(s_self - peak)
    denominator = jnp.sum(e_cache, axis=2) + e_self
    p_cache = (e_cache / denominator[:, :, None]).astype(jnp.bfloat16)
    p_self = (e_self / denominator).astype(jnp.bfloat16)
    context = jnp.einsum('ths,tsc->thc', p_cache, ckv_cache, preferred_element_type=jnp.float32) + p_self.astype(jnp.float32)[:, :, None] * c_new.astype(jnp.float32)[:, None, :]
    heads_out = jnp.einsum('thc,chv->thv', context.astype(jnp.bfloat16), w_uv.reshape(kv_rank, heads, VALUE_DIM), preferred_element_type=jnp.float32).astype(jnp.bfloat16)
    attn_out = jnp.dot(heads_out.reshape(tokens, heads * VALUE_DIM), w_out, preferred_element_type=jnp.float32)
    x_mid = (hidden.astype(jnp.float32) + attn_out).astype(jnp.bfloat16)
    return x_mid, c_new, k_new


def route_weights(u_norm, topk_ids, w_router, capacity):
    experts = w_router.shape[1]
    gates = jax.nn.sigmoid(jnp.dot(u_norm, w_router, preferred_element_type=jnp.float32))
    chosen = jnp.take_along_axis(gates, topk_ids, axis=1)
    weights = ROUTE_SCALE * chosen / jnp.sum(chosen, axis=1, keepdims=True)
    hits = (topk_ids[:, :, None] == jnp.arange(experts)[None, None, :]).astype(jnp.int32)
    per_token = jnp.sum(hits, axis=1)
    before = jnp.cumsum(per_token, axis=0) - per_token
    rank = jnp.sum(hits * before[:, None, :], axis=2)
    keep = rank < capacity
    slots = jnp.where(keep, topk_ids * capacity + rank, -1)
    return jnp.where(keep, weights, 0.0), slots


def expert_block(rows, w_gate, w_up, w_down):
    h_gate = jnp.einsum('slcd,ldf->slcf', rows, w_gate, preferred_element_type=jnp.float32)
    h_up = jnp.einsum('slcd,ldf->slcf', rows, w_up, preferred_element_type=jnp.float32)
    act = (jax.nn.silu(h_gate) * h_up).astype(jnp.bfloat16)
    return jnp.einsum('slcf,lfd->slcd', act, w_down, preferred_element_type=jnp.float32).astype(jnp.bfloat16)


def shared_block(u_norm, shared_gate, shared_up, shared_down):
    h_gate = jnp.dot(u_norm, shared_gate, preferred_element_type=jnp.float32)
    h_up = jnp.dot(u_norm, shared_up, preferred_element_type=jnp.float32)
    act = (jax.nn.silu(h_gate) * h_up).astype(jnp.bfloat16)
    return jnp.dot(act, shared_down, preferred_element_type=jnp.float32).astype(jnp.bfloat16)


def solution(mesh):
    ep_size = mesh.shape['ep']
    batch = P(('dp', 'ep'))
    whole = P()
    by_expert = P('ep')

    def local_step(hidden, positions, ckv_cache, kpe_cache, topk_ids, attn_gain, w_dq, q_gain, w_uq, w_dkv, kv_gain, w_uk, w_uv, w_out, ffn_gain, w_router, w_gate, w_up, w_down, shared_gate, shared_up, shared_down):
        x_mid, c_new, k_new = attention_block(hidden, positions, ckv_cache, kpe_cache, attn_gain, w_dq, q_gain, w_uq, w_dkv, kv_gain, w_uk, w_uv, w_out)
        u_norm = rms_norm(x_mid, ffn_gain).astype(jnp.bfloat16)
        tokens, width = u_norm.shape
        experts = w_router.shape[1]
        local = w_gate.shape[0]
        capacity = (CAP_FACTOR * tokens * topk_ids.shape[1] + experts - 1) // experts
        weights, slots = route_weights(u_norm, topk_ids, w_router, capacity)
        route_mat = jnp.any(slots[:, :, None] == jnp.arange(experts * capacity)[None, None, :], axis=1).astype(jnp.bfloat16)
        outgoing = jnp.einsum('tm,td->md', route_mat, u_norm, preferred_element_type=jnp.float32).astype(jnp.bfloat16)
        incoming = lax.all_to_all(outgoing, 'ep', 0, 0, tiled=True).reshape(ep_size, local, capacity, width)
        results = expert_block(incoming, w_gate, w_up, w_down).reshape(ep_size * local * capacity, width)
        returned = lax.all_to_all(results, 'ep', 0, 0, tiled=True)
        picked = jnp.take(returned, jnp.maximum(slots, 0), axis=0)
        routed = jnp.sum(weights[:, :, None] * picked.astype(jnp.float32), axis=1)
        shared_out = shared_block(u_norm, shared_gate, shared_up, shared_down)
        hidden_out = (x_mid.astype(jnp.float32) + routed + shared_out.astype(jnp.float32)).astype(jnp.bfloat16)
        return hidden_out, c_new, k_new

    in_specs = (batch,) * 5 + (whole,) * 11 + (by_expert,) * 3 + (whole,) * 3
    return jax.shard_map(local_step, mesh=mesh, in_specs=in_specs, out_specs=(batch, batch, batch), check_vma=False)
```

profile of v0, /device:TPU:112, one launch (start us, length us, event | category | flops | bytes accessed | tf_op | source)
XLA Modules:
  0.0 645.9 jit_solution(7834354042921111108)
XLA Ops:
  0.7 0.8 convert_element_type.127
  1.5 1.4 iota_compare_fusion.1
  2.8 0.7 convert_element_type.119
  3.5 1.7 fusion.25
  5.2 4.8 fusion.57
  10.5 0.8 subtract_convert_fusion.1
  11.4 0.8 copy.65
  12.2 8.4 %multiply_reduce_fusion.2 = (f32[128]{0:T(128)S(1)}, f32[128,1536]{1,0:T(8,128)S(1)}) fusion(bf16[5120,1536]{1,0:T(8,128)(2,1)} %param.28, bf16[128,5120]{1,0:T(8,128)(2,1)} %param.22, f32[5120]{0:T(1024)} %copy-done.14, f32[128]{0:T(128)} %copy-done.32), kind=kOutput, calls=%fused_computation.70 | convolution fusion | flops 2016280448 | bytes 17847296 | tf_op jit(solution)/shard_map/dot_general | solution.py:39
  20.6 2.4 convolution_convert_fusion.2
  23.0 1.5 copy.59
  24.5 0.8 copy-done.6
  25.4 1.2 copy.90
  26.6 1.1 convert_element_type.126
  27.7 0.6 fusion.88
  28.3 1.5 copy.83
  29.8 3.1 convert_bitcast_fusion.1
  32.9 0.9 copy.81
  33.8 15.3 %fusion.38 = f32[128,16,256]{2,1,0:T(8,128)S(1)} fusion(bf16[128,256,512]{2,1,0:T(8,128)(2,1)} %param.24, bf16[128,16,512]{2,0,1:T(8,128)(2,1)} %convert_bitcast_fusion.1), kind=kOutput, calls=%fused_computation.52 | convolution fusion | flops 536870912 | bytes 37748736 | tf_op jit(solution)/shard_map/thc,tsc->ths/dot_general | solution.py:48
  49.2 1.4 fusion.36
  50.6 0.5 subtract_convert_fusion
  51.1 0.5 fusion.61
  51.5 1.2 copy-done.5
  52.8 1.1 fusion.70
  53.9 0.6 fusion.35
  54.7 3.9 copy.88
  58.6 13.3 %add_convert_fusion = bf16[128,16,512]{2,1,0:T(8,128)(2,1)S(1)} fusion(f32[128,512]{1,0:T(8,128)S(1)} %copy.66, f32[128,16]{1,0:T(8,128)S(1)} %get-tuple-element.19, bf16[128,256,512]{2,1,0:T(8,128)(2,1)} %param.24, f32[128,16,256]{2,1,0:T(8,128)S(1)} %get-tuple-element.25, f32[128,16]{1,0:T(8,128)S(1)} %get-tuple-element.18, f32[128,16]{1,0:T(8,128)S(1)} %fusion.63), kind=kOutput, calls=%fused_computation.29 | convolution fusion | flops 541589504 | bytes 38035456 | tf_op jit(solution)/shard_map/ths,tsc->thc/dot_general | solution.py:58
  71.9 1.5 fusion.45
  73.5 11.7 %multiply_reduce_fusion.1 = (f32[128]{0:T(128)S(1)}, f32[128,5120]{1,0:T(8,128)}) fusion(bf16[128,2048]{0,1:T(8,128)(2,1)S(1)} %bitcast.96, bf16[2048,5120]{1,0:T(8,128)(2,1)} %param.35, bf16[128,5120]{1,0:T(8,128)(2,1)S(1)} %copy-done.3), kind=kOutput, calls=%fused_computation.39 | convolution fusion | flops 2688286720 | bytes 25428480 | tf_op jit(solution)/shard_map/dot_general | solution.py:60
  85.6 0.6 broadcast_compare_fusion
  86.2 0.8 fusion.23
  87.0 9.6 %convolution_convert_fusion = bf16[1536,5120]{1,0:T(8,128)(2,1)} fusion(pred[128,1536]{1,0:T(8,128)(4,1)S(1)} %fusion.23, f32[128,5120]{1,0:T(8,128)} %get-tuple-element.27, f32[5120]{0:T(1024)S(1)} %convert_element_type.141, f32[128]{0:T(128)S(1)} %add_rsqrt_fusion), kind=kOutput, calls=%fused_computation.9 | convolution fusion | flops 2023096320 | bytes 18567680 | tf_op jit(solution)/shard_map/tm,td->md/dot_general | solution.py:108
  96.6 178.9 %all_to_all.21 = bf16[8,192,5120]{2,1,0:T(8,128)(2,1)S(1)} all-to-all(bf16[8,192,5120]{2,1,0:T(8,128)(2,1)} %bitcast.87), channel_id=1, replica_groups=mesh['dp'=2,'ep'=8] {'ep'}, dimensions={0} | all-to-all | bytes 31457280 | tf_op jit(solution)/shard_map/all_to_all | solution.py:109
  275.5 5.5 copy-done.2
  280.9 29.8 %fusion.4 = f32[2,8,96,1536]{3,2,1,0:T(8,128)} fusion(bf16[2,5120,1536]{2,1,0:T(8,128)(2,1)} %param.38, bf16[8,2,96,5120]{3,2,1,0:T(8,128)(2,1)S(1)} %bitcast.91), kind=kOutput, calls=%fused_computation.6 | convolution fusion | flops 24159191040 | bytes 56623104 | tf_op jit(solution)/shard_map/slcd,ldf->slcf/dot_general | solution.py:80
  310.7 33.0 %fusion.10 = bf16[8,2,96,1536]{3,2,0,1:T(8,128)(2,1)} fusion(f32[2,8,96,1536]{3,2,1,0:T(8,128)} %fusion.4, bf16[2,5120,1536]{2,1,0:T(8,128)(2,1)} %param.39, bf16[8,2,96,5120]{3,2,1,0:T(8,128)(2,1)} %bitcast.92), kind=kOutput, calls=%fused_computation.14 | convolution fusion | flops 24173346816 | bytes 61341696 | tf_op jit(solution)/shard_map/slcd,ldf->slcf/dot_general | solution.py:81
  343.7 31.8 %convert_bitcast_fusion = bf16[8,2,96,5120]{3,2,0,1:T(8,128)(2,1)} fusion(bf16[8,2,96,1536]{3,2,0,1:T(8,128)(2,1)} %fusion.10, bf16[2,1536,5120]{2,1,0:T(8,128)(2,1)} %param.40), kind=kOutput, calls=%fused_computation.10 | convolution fusion | flops 24167055360 | bytes 51904512 | tf_op jit(solution)/shard_map/slcf,lfd->slcd/dot_general | solution.py:83
  375.5 13.2 %copy.78 = bf16[8,2,96,5120]{3,2,1,0:T(8,128)(2,1)} copy(bf16[8,2,96,5120]{3,2,0,1:T(8,128)(2,1)} %convert_bitcast_fusion) | data formatting | bytes 31457280 | tf_op jit(solution)/shard_map/convert_element_type | solution.py:83
  388.8 6.0 all-to-all-start.1
  394.8 0.8 copy.80
  396.2 2.3 fusion.50
  398.5 5.1 gather_fusion.1
  404.1 0.6 pad_maximum_fusion.3
  404.7 16.2 %fusion.69 = f32[128,3072]{1,0:T(8,128)} fusion(bf16[5120,3072]{1,0:T(8,128)(2,1)} %param.41, f32[128,5120]{1,0:T(8,128)} %get-tuple-element.27, f32[5120]{0:T(1024)S(1)} %copy-done.11, f32[128]{0:T(128)S(1)} %copy-done.28), kind=kOutput, calls=%fused_computation.113 | convolution fusion | flops 4028497920 | bytes 35672576 | tf_op jit(solution)/shard_map/dot_general | solution.py:87
  420.9 146.9 %all-to-all-done.1 = bf16[8,192,5120]{2,1,0:T(8,128)(2,1)} async-done(((bf16[8,192,5120]{2,1,0:T(8,128)(2,1)}), bf16[8,192,5120]{2,1,0:T(8,128)(2,1)}, u32[]{:S(2)}, u32[]{:S(2)}) %all-to-all-start.1) | async-done | bytes 15728672 | tf_op jit(solution)/shard_map/all_to_all | solution.py:111
  567.8 22.4 %gather_fusion = bf16[768,5120]{1,0:T(8,128)(2,1)} fusion(bf16[1536,5120]{1,0:T(8,128)(2,1)} %bitcast.24, s32[1024]{0:T(1024)S(1)} %pad_clamp_fusion), kind=kCustom, calls=%fused_computation | custom fusion | bytes 15731712 | tf_op jit(solution)/shard_map/jit(_take)/gather | solution.py:112
  590.3 13.1 %reshape.207 = bf16[128,6,5120]{2,1,0:T(8,128)(2,1)} reshape(bf16[768,5120]{1,0:T(8,128)(2,1)} %gather_fusion) | data formatting | bytes 15728640 | tf_op jit(solution)/shard_map/jit(_take)/gather | solution.py:112
  603.4 12.2 %multiply_reduce_fusion = f32[128,5120]{1,0:T(8,128)} fusion(bf16[128,6,5120]{2,1,0:T(8,128)(2,1)} %reshape.207, f32[128,6]{1,0:T(8,128)S(1)} %copy.74, pred[128,6]{1,0:T(8,128)(4,1)S(1)} %copy.75), kind=kLoop, calls=%fused_computation.8 | loop fusion | flops 15073280 | bytes 10489600 | tf_op jit(solution)/shard_map/reduce_sum | solution.py:113
  615.6 30.1 %fusion.17 = bf16[128,5120]{1,0:T(8,128)(2,1)} fusion(bf16[3072,5120]{1,0:T(8,128)(2,1)} %param.43, bf16[5120,3072]{1,0:T(8,128)(2,1)} %param.42, f32[128,5120]{1,0:T(8,128)} %get-tuple-element.27, f32[128,5120]{1,0:T(8,128)} %multiply_reduce_fusion, f32[128,3072]{1,0:T(8,128)} %fusion.69, f32[5120]{0:T(1024)S(1)} %copy-done.11, f32[128]{0:T(128)S(1)} %copy-done.28), kind=kOutput, calls=%fused_computation.25 | convolution fusion | flops 8060665856 | bytes 71062016 | tf_op jit(solution)/shard_map/dot_general | solution.py:90
  (107 shorter events, 2.3 us)
Async XLA Ops:
  0.6 29.2 %copy-start = (bf16[512,2048]{1,0:T(8,128)(2,1)S(1)}, bf16[512,2048]{1,0:T(8,128)(2,1)}, u32[]{:S(2)}) copy-start(bf16[512,2048]{1,0:T(8,128)(2,1)} %param.33) | copy-start | bytes 6291460
  3.5 6.5 %copy-start.14 = (f32[5120]{0:T(1024)}, f32[5120]{0:T(1024)S(1)}, u32[]{:S(2)}) copy-start(f32[5120]{0:T(1024)S(1)} %convert_element_type.119) | copy-start | bytes 61444
  5.2 4.9 copy-start.32
  5.2 5.0 copy-start.33
  10.3 10.3 %slice-start = ((s8[9437184]{0:T(1024)(128)(4,1)}), s8[1048576]{0:T(1024)(128)(4,1)S(1)}, s32[]{:S(2)}) async-start(s8[9437184]{0:T(1024)(128)(4,1)} %bitcast.89), calls=%async_computation.2 | async-start | bytes 2097152
  10.5 44.1 %copy-start.8 = (bf16[128,512]{0,1:T(8,128)(2,1)}, bf16[128,512]{0,1:T(8,128)(2,1)S(1)}, u32[]{:S(2)}) copy-start(bf16[128,512]{0,1:T(8,128)(2,1)S(1)} %multiply_convert_fusion.3) | copy-start | bytes 393220
  11.3 16.5 %copy-start.19 = (bf16[128,32]{0,1:T(8,128)(2,1)}, bf16[128,32]{0,1:T(8,128)(2,1)S(1)}, u32[]{:S(2)}) copy-start(bf16[128,32]{0,1:T(8,128)(2,1)S(1)} %get-tuple-element.16) | copy-start | bytes 24580
  11.3 16.5 %copy-start.21 = (bf16[128,32]{0,1:T(8,128)(2,1)}, bf16[128,32]{0,1:T(8,128)(2,1)S(1)}, u32[]{:S(2)}) copy-start(bf16[128,32]{0,1:T(8,128)(2,1)S(1)} %get-tuple-element.17) | copy-start | bytes 24580
  12.2 8.4 %copy-start.30 = (bf16[1536]{0:T(1024)(128)(2,1)S(1)}, bf16[1536]{0:T(1024)(128)(2,1)}, u32[]{:S(2)}) copy-start(bf16[1536]{0:T(1024)(128)(2,1)} %param.29) | copy-start | bytes 9220
  12.2 8.4 %slice-start.1 = ((s8[9437184]{0:T(1024)(128)(4,1)}), s8[4194304]{0:T(1024)(128)(4,1)S(1)}, s32[]{:S(2)}) async-start(s8[9437184]{0:T(1024)(128)(4,1)} %bitcast.89), calls=%async_computation.3 | async-start | bytes 8388608
  12.2 8.4 %slice-start.2 = ((s8[9437184]{0:T(1024)(128)(4,1)}), s8[4194304]{0:T(1024)(128)(4,1)S(1)}, s32[]{:S(2)}) async-start(s8[9437184]{0:T(1024)(128)(4,1)} %bitcast.89), calls=%async_computation.4 | async-start | bytes 8388608
  24.5 0.9 copy-start.6
  33.8 15.3 %copy-start.4 = (bf16[128,16,512]{2,0,1:T(8,128)(2,1)S(1)}, bf16[128,16,512]{2,0,1:T(8,128)(2,1)}, u32[]{:S(2)}) copy-start(bf16[128,16,512]{2,0,1:T(8,128)(2,1)} %convert_bitcast_fusion.1) | copy-start | bytes 6291460
  33.8 15.3 %copy-start.13 = (bf16[128,512,1]{1,2,0:T(2,128)(2,1)S(1)}, bf16[128,512,1]{1,2,0:T(2,128)(2,1)}, u32[]{:S(2)}) copy-start(bf16[128,512,1]{1,2,0:T(2,128)(2,1)} %copy.81) | copy-start | bytes 393220
  49.2 1.9 copy-start.12
  50.6 2.2 copy-start.5
  50.6 2.2 copy-start.18
  58.6 13.3 %copy-start.7 = (bf16[512,2048]{0,1:T(8,128)(2,1)S(1)}, bf16[512,2048]{0,1:T(8,128)(2,1)}, u32[]{:S(2)}) copy-start(bf16[512,2048]{0,1:T(8,128)(2,1)} %copy.88) | copy-start | bytes 6291460
  71.9 1.5 copy-start.3
  73.4 11.7 %copy-start.16 = (s32[128,6]{0,1:T(8,128)S(1)}, s32[128,6]{0,1:T(8,128)}, u32[]{:S(2)}) copy-start(s32[128,6]{0,1:T(8,128)} %param.26) | copy-start | bytes 9220
  73.4 13.5 %copy-start.29 = (bf16[5120]{0:T(1024)(128)(2,1)S(1)}, bf16[5120]{0:T(1024)(128)(2,1)}, u32[]{:S(2)}) copy-start(bf16[5120]{0:T(1024)(128)(2,1)} %param.36) | copy-start | bytes 30724
  85.2 11.4 %copy-start.27 = (f32[128]{0:T(128)}, f32[128]{0:T(128)S(1)}, u32[]{:S(2)}) copy-start(f32[128]{0:T(128)S(1)} %add_rsqrt_fusion) | copy-start | bytes 1540
  85.6 11.0 %copy-start.25 = (s32[128,6]{0,1:T(8,128)}, s32[128,6]{0,1:T(8,128)S(1)}, u32[]{:S(2)}) copy-start(s32[128,6]{0,1:T(8,128)S(1)} %select_reduce_fusion) | copy-start | bytes 9220
  86.2 10.4 %copy-start.23 = (s32[128,6]{0,1:T(8,128)}, s32[128,6]{0,1:T(8,128)S(1)}, u32[]{:S(2)}) copy-start(s32[128,6]{0,1:T(8,128)S(1)} %get-tuple-element.13) | copy-start | bytes 9220
  87.0 9.6 %copy-start.10 = (f32[5120]{0:T(1024)}, f32[5120]{0:T(1024)S(1)}, u32[]{:S(2)}) copy-start(f32[5120]{0:T(1024)S(1)} %convert_element_type.141) | copy-start | bytes 61444
  275.5 5.5 copy-start.2
  388.8 6.0 copy-start.9
  388.8 6.8 %copy-start.24 = (s32[128,6]{0,1:T(8,128)S(1)}, s32[128,6]{0,1:T(8,128)}, u32[]{:S(2)}) copy-start(s32[128,6]{0,1:T(8,128)} %copy-done.23) | copy-start | bytes 9220
  388.8 7.1 %copy-start.17 = (s32[128,6]{0,1:T(8,128)S(1)}, s32[128,6]{0,1:T(8,128)}, u32[]{:S(2)}) copy-start(s32[128,6]{0,1:T(8,128)} %param.26) | copy-start | bytes 9220
  388.8 7.3 %copy-start.11 = (f32[5120]{0:T(1024)S(1)}, f32[5120]{0:T(1024)}, u32[]{:S(2)}) copy-start(f32[5120]{0:T(1024)} %copy-done.10) | copy-start | bytes 61444
  388.8 7.3 %copy-start.15 = (bf16[5120,16]{0,1:T(8,128)(2,1)S(1)}, bf16[5120,16]{0,1:T(8,128)(2,1)}, u32[]{:S(2)}) copy-start(bf16[5120,16]{0,1:T(8,128)(2,1)} %param.37) | copy-start | bytes 491524
  388.8 7.3 %copy-start.28 = (f32[128]{0:T(128)S(1)}, f32[128]{0:T(128)}, u32[]{:S(2)}) copy-start(f32[128]{0:T(128)} %copy-done.27) | copy-start | bytes 1540
  388.8 179.0 %all-to-all-start.1 = ((bf16[8,192,5120]{2,1,0:T(8,128)(2,1)}), bf16[8,192,5120]{2,1,0:T(8,128)(2,1)}, u32[]{:S(2)}, u32[]{:S(2)}) async-start(bf16[8,192,5120]{2,1,0:T(8,128)(2,1)} %bitcast.88), calls=%async_computation.1 | async-start | bytes 31457280 | tf_op jit(solution)/shard_map/all_to_all | solution.py:111
  398.4 5.4 copy-start.26
  398.4 5.5 copy-start.31
  398.4 5.7 copy-start.20
  398.5 5.7 copy-start.22
  615.6 30.1 %copy-start.1 = (bf16[512,2048]{1,0:T(8,128)(2,1)S(1)}, bf16[512,2048]{1,0:T(8,128)(2,1)}, u32[]{:S(2)}) copy-start(bf16[512,2048]{1,0:T(8,128)(2,1)} %param.33) | copy-start | bytes 6291460
where the time goes:
time: 653 us; the launch traced here: 646 us
  matrix products  216 us (33%)
  blocking collectives  179 us (27%)
  waiting for transfers between devices  147 us (23%)
  local copies, waits for them, and re-layouts  73.5 us (11%)
  other arithmetic  23 us (4%)
    all_to_all x1, blocking collectives, local_step(): lax.all_to_all(outgoing, 'ep', 0, 0, tiled=True)  179 us
    all_to_all x1, waiting for transfers between devices, local_step(): returned = lax.all_to_all(results, 'ep', 0, 0, tiled=True)  147 us
    gather x2, local copies, waits for them, and re-layouts, local_step(): picked = jnp.take(returned, jnp.maximum(slots, 0), axis=0)  35.5 us
    dot_general x1, matrix products, expert_block(): jnp.einsum('slcd,ldf->slcf', rows, w_up, preferred_element_type=jnp.float32)  33 us
    dot_general x1, matrix products, expert_block(): jnp.einsum('slcf,lfd->slcd', act, w_down, preferred_element_type=jnp.floa...  31.8 us
    dot_general x1, matrix products, shared_block(): jnp.dot(act, shared_down, preferred_element_type=jnp.float32)  30.1 us
    dot_general x1, matrix products, expert_block(): jnp.einsum('slcd,ldf->slcf', rows, w_gate, preferred_element_type=jnp.flo...  29.8 us
    dot_general x1, matrix products, shared_block(): h_gate = jnp.dot(u_norm, shared_gate, preferred_element_type=jnp.float32)  16.2 us
  transfers between devices with their start and end apart: 1, of which 1 were waited for; matrix products, arithmetic and copies ran while one was open for 4% of the time, Pallas kernels for 0%

commit v1 on v0

--- a/solution.py
+++ b/solution.py
@@ -1,6 +1,10 @@
+import functools
+
 import jax
 import jax.numpy as jnp
 from jax import lax
+from jax.experimental import pallas as pl
+from jax.experimental.pallas import tpu as pltpu
 from jax.sharding import PartitionSpec as P
 
 NOPE_DIM = 128
@@ -11,6 +15,10 @@
 ROUTE_SCALE = 2.5
 ROPE_BASE = 10000.0
 CAP_FACTOR = 2
+CORES = 2
+F_TILE = 256
+D_TILE = 512
+MESH = pl.DeviceIdType.MESH
 
 
 def rms_norm(vec, gain):
@@ -62,32 +70,382 @@
     return x_mid, c_new, k_new
 
 
-def route_weights(u_norm, topk_ids, w_router, capacity):
+def route_table(u_norm, topk_ids, w_router, local, capacity):
+    tokens = u_norm.shape[0]
     experts = w_router.shape[1]
     gates = jax.nn.sigmoid(jnp.dot(u_norm, w_router, preferred_element_type=jnp.float32))
-    chosen = jnp.take_along_axis(gates, topk_ids, axis=1)
-    weights = ROUTE_SCALE * chosen / jnp.sum(chosen, axis=1, keepdims=True)
-    hits = (topk_ids[:, :, None] == jnp.arange(experts)[None, None, :]).astype(jnp.int32)
-    per_token = jnp.sum(hits, axis=1)
-    before = jnp.cumsum(per_token, axis=0) - per_token
-    rank = jnp.sum(hits * before[:, None, :], axis=2)
-    keep = rank < capacity
-    slots = jnp.where(keep, topk_ids * capacity + rank, -1)
-    return jnp.where(keep, weights, 0.0), slots
-
-
-def expert_block(rows, w_gate, w_up, w_down):
-    h_gate = jnp.einsum('slcd,ldf->slcf', rows, w_gate, preferred_element_type=jnp.float32)
-    h_up = jnp.einsum('slcd,ldf->slcf', rows, w_up, preferred_element_type=jnp.float32)
-    act = (jax.nn.silu(h_gate) * h_up).astype(jnp.bfloat16)
-    return jnp.einsum('slcf,lfd->slcd', act, w_down, preferred_element_type=jnp.float32).astype(jnp.bfloat16)
-
-
-def shared_block(u_norm, shared_gate, shared_up, shared_down):
-    h_gate = jnp.dot(u_norm, shared_gate, preferred_element_type=jnp.float32)
-    h_up = jnp.dot(u_norm, shared_up, preferred_element_type=jnp.float32)
-    act = (jax.nn.silu(h_gate) * h_up).astype(jnp.bfloat16)
-    return jnp.dot(act, shared_down, preferred_element_type=jnp.float32).astype(jnp.bfloat16)
+    hits = jnp.any(topk_ids[:, :, None] == jnp.arange(experts), axis=1)
+    total = jnp.sum(jnp.where(hits, gates, 0.0), axis=1, keepdims=True)
+    group_hits = hits[:, ::local]
+    earlier = (jnp.arange(tokens)[:, None] > jnp.arange(tokens)[None, :]).astype(jnp.bfloat16)
+    rank = jnp.dot(earlier, group_hits.astype(jnp.bfloat16), preferred_element_type=jnp.float32)
+    slots = jnp.where(group_hits & (rank < capacity), rank, -1.0)
+    weights = jnp.where(hits, ROUTE_SCALE * gates / total, 0.0)
+    table = jnp.concatenate([weights, slots], axis=1).T
+    return jnp.pad(table, ((0, -table.shape[0] % 8), (0, 0)))
+
+
+def moe_kernel(chips, capacity, u_ref, mid_ref, table_ref, gate_ref, up_ref, down_ref, sgate_ref, sup_ref, sdown_ref, out_ref,
+               far_u, picked, act, wbuf, eout, agg, stage, landed, one_in, two_plus, two_minus, tables, scales, spread, shared,
+               w_sem, table_send, table_recv, u_send, u_recv, pair_send, pair_recv, near_send, one_send, one_recv, two_send, plus_recv, minus_recv, credit):
+    tokens, width = u_ref.shape
+    local, _, ff = gate_ref.shape
+    experts = local * chips * CORES
+    half = tokens // 2
+    f_blocks = ff // F_TILE
+    steps_f = local * f_blocks
+    steps_d = width // D_TILE
+    cols = D_TILE // F_TILE
+    me = lax.axis_index('ep')
+    chip = lax.div(me, CORES)
+    core = lax.rem(me, CORES)
+
+    def peer(offset, other):
+        return lax.rem(chip + offset, chips) * CORES + (1 - core if other else core)
+
+    def remote(src, dst, send_sem, recv_sem, offset, other):
+        return pltpu.make_async_remote_copy(src_ref=src, dst_ref=dst, send_sem=send_sem, recv_sem=recv_sem, device_id={'ep': peer(offset, other)}, device_id_type=MESH)
+
+    plus, minus, far = 1, chips - 1, chips // 2
+    peers = [(o, q) for q in range(CORES) for o in range(chips) if (o, q) != (0, 0)]
+
+    def u_at(offset, other):
+        index = other * chips + offset
+        return u_ref if index == 0 else far_u.at[index - 1]
+
+    def expert_in(step, slot):
+        e, b = lax.div(step, f_blocks), lax.rem(step, f_blocks)
+        at = pl.ds(pl.multiple_of(b * F_TILE, F_TILE), F_TILE)
+        return [pltpu.make_async_copy(ref.at[e, :, at], wbuf.at[slot, k], w_sem.at[slot, k]) for k, ref in enumerate((gate_ref, up_ref))]
+
+    def shared_in(step, slot):
+        at = pl.ds(pl.multiple_of(step * F_TILE, F_TILE), F_TILE)
+        return [pltpu.make_async_copy(ref.at[:, at], wbuf.at[slot, k], w_sem.at[slot, k]) for k, ref in enumerate((sgate_ref, sup_ref))]
+
+    def down_copies(piece, step, slot):
+        copies = []
+        for e in range(local):
+            for h in range(cols):
+                at = pl.ds(pl.multiple_of(step * D_TILE + h * F_TILE, F_TILE), F_TILE)
+                copies.append(pltpu.make_async_copy(piece(e, at), wbuf.at[slot, e, pl.ds(h * ff, ff)], w_sem.at[slot, e * cols + h]))
+        return copies
+
+    def expert_out(step, slot):
+        return down_copies(lambda e, at: down_ref.at[e, :, at], step, slot)
+
+    def shared_down(step, slot):
+        return down_copies(lambda e, at: sdown_ref.at[pl.ds(e * ff, ff), at], step, slot)
+
+    def begin(copies):
+        for copy in copies:
+            copy.start()
+
+    def finish(copies):
+        for copy in copies:
+            copy.wait()
+
+    def stream(step, steps, load, following):
+        slot = lax.rem(step, 2)
+
+        @pl.when(step < steps - 1)
+        def _():
+            begin(load(step + 1, 1 - slot))
+
+        if following is not None:
+            @pl.when(step == steps - 1)
+            def _():
+                begin(following(0, 0))
+
+        finish(load(step, slot))
+        return slot
+
+    def gate_up(lhs, load, following):
+        rows = lhs.shape[0]
+
+        def body(step, carry):
+            slot = stream(step, steps_f, load, following)
+            e, b = lax.div(step, f_blocks), lax.rem(step, f_blocks)
+            h_gate = jnp.dot(lhs[...], wbuf[slot, 0], preferred_element_type=jnp.float32)
+            h_up = jnp.dot(lhs[...], wbuf[slot, 1], preferred_element_type=jnp.float32)
+            act[e, pl.ds(0, rows), pl.ds(pl.multiple_of(b * F_TILE, F_TILE), F_TILE)] = (h_gate * jax.nn.sigmoid(h_gate) * h_up).astype(jnp.bfloat16)
+            return carry
+
+        lax.fori_loop(0, steps_f, body, 0)
+
+    begin(shared_in(0, 0))
+    barrier = pltpu.get_barrier_semaphore()
+    for o, q in peers:
+        pl.semaphore_signal(barrier, inc=1, device_id={'ep': peer(o, q)}, device_id_type=MESH)
+    pl.semaphore_wait(barrier, len(peers))
+
+    def table_copy(k):
+        o, q = peers[k]
+        back = q * chips + (chips - o) % chips
+        return remote(table_ref, tables.at[back], table_send.at[k], table_recv.at[back], o, q)
+
+    for k in range(len(peers)):
+        table_copy(k).start()
+
+    top, low = pl.ds(0, half), pl.ds(half, half)
+    routes = [
+        (u_at(0, 0), u_at(0, 1), 0, 1),
+        (u_at(0, 0), u_at(minus, 0), plus, 0),
+        (u_at(0, 0), u_at(plus, 0), minus, 0),
+        (u_at(minus, 0), u_at(minus, 1), 0, 1),
+        (u_at(minus, 0).at[top], u_at(far, 0).at[top], plus, 0),
+        (u_at(plus, 0), u_at(plus, 1), 0, 1),
+        (u_at(plus, 0).at[low], u_at(far, 0).at[low], minus, 0),
+        (u_at(far, 0).at[top], u_at(far, 1).at[top], 0, 1),
+        (u_at(far, 0).at[low], u_at(far, 1).at[low], 0, 1),
+    ]
+
+    def u_copy(k):
+        src, dst, o, q = routes[k]
+        return remote(src, dst, u_send.at[k], u_recv.at[k], o, q)
+
+    for k in (1, 2, 0):
+        u_copy(k).start()
+
+    gate_up(u_ref, shared_in, shared_down)
+
+    def shared_body(step, carry):
+        slot = stream(step, steps_d, shared_down, expert_in)
+        for h in range(cols):
+            total = None
+            for e in range(local):
+                piece = jnp.dot(act[e, pl.ds(0, tokens), :], wbuf[slot, e, pl.ds(h * ff, ff), :], preferred_element_type=jnp.float32)
+                total = piece if total is None else total + piece
+            shared[:, pl.ds(pl.multiple_of(step * D_TILE + h * F_TILE, F_TILE), F_TILE)] = total.astype(jnp.bfloat16)
+        return carry
+
+    lax.fori_loop(0, steps_d, shared_body, 0)
+
+    u_copy(1).wait_recv()
+    u_copy(4).start()
+    u_copy(3).start()
+    u_copy(2).wait_recv()
+    u_copy(6).start()
+    u_copy(5).start()
+    for k in range(len(peers)):
+        table_copy(k).wait_recv()
+    tables[0] = table_ref[...]
+
+    def place_tables(index):
+        slot_row = tables[index, pl.ds(experts + me, 1), :]
+        slot_col = jnp.transpose(jnp.broadcast_to(slot_row, (tokens, tokens)))
+        lane = lax.broadcasted_iota(jnp.int32, (tokens, tokens), 1).astype(jnp.float32)
+        spread[index] = jnp.where(slot_col == lane, 1.0, 0.0).astype(jnp.bfloat16)[:, :capacity]
+        for e in range(local):
+            row = tables[index, pl.ds(me * local + e, 1), :]
+            scales[index, e] = jnp.transpose(jnp.broadcast_to(row, (tokens, tokens)))
+
+    def pick(sources):
+        for i, (o, q) in enumerate(sources):
+            index = q * chips + o
+            place_tables(index)
+            slot_row = tables[index, pl.ds(experts + me, 1), :]
+            line = lax.broadcasted_iota(jnp.int32, (capacity, tokens), 0).astype(jnp.float32)
+            place = jnp.where(slot_row == line, 1.0, 0.0).astype(jnp.bfloat16)
+            source = u_at(o, q)
+
+            def body(step, carry, i=i, place=place, source=source):
+                at = pl.ds(pl.multiple_of(step * D_TILE, D_TILE), D_TILE)
+                picked[pl.ds(i * capacity, capacity), at] = jnp.dot(place, source[:, at], preferred_element_type=jnp.float32).astype(jnp.bfloat16)
+                return carry
+
+            lax.fori_loop(0, steps_d, body, 0)
+
+    def pair_copy(step):
+        slot = lax.rem(step, 2)
+        return remote(stage.at[slot], landed.at[step], pair_send.at[slot], pair_recv.at[step], 0, 1)
+
+    def down(sources, offsets, following, pass_on):
+        def body(step, carry):
+            @pl.when((step >= 1) & (step <= steps_d))
+            def _():
+                pair_copy(step - 1).start()
+
+            @pl.when(step < steps_d)
+            def _():
+                slot = stream(step, steps_d, expert_out, following)
+                for e in range(local):
+                    for h in range(cols):
+                        eout[e, :, pl.ds(h * F_TILE, F_TILE)] = jnp.dot(act[e], wbuf[slot, e, pl.ds(h * ff, ff), :], preferred_element_type=jnp.float32).astype(jnp.bfloat16)
+
+                @pl.when(step >= 2)
+                def _():
+                    pair_copy(step - 2).wait_send()
+
+                for i, (o, q) in enumerate(sources):
+                    index = q * chips + o
+                    for h in range(cols):
+                        at = pl.ds(h * F_TILE, F_TILE)
+                        total = None
+                        for e in range(local):
+                            scale = jnp.concatenate([scales[index, e]] * (F_TILE // tokens), axis=1)
+                            piece = jnp.dot(spread[index], eout[e, pl.ds(i * capacity, capacity), at], preferred_element_type=jnp.float32) * scale
+                            total = piece if total is None else total + piece
+                        if q == 0:
+                            agg[o, step, :, at] = total
+                        else:
+                            stage[slot, offsets.index(o), :, at] = total
+
+            @pl.when((step >= 2) & (step <= steps_d + 1))
+            def _():
+                block = step - 2
+                pair_copy(block).wait_recv()
+                for k, o in enumerate(offsets):
+                    agg[o, block] = agg[o, block] + landed[block, k]
+
+            @pl.when(step >= 3)
+            def _():
+                pass_on(step - 3)
+
+            return carry
+
+        lax.fori_loop(0, steps_d + 3, body, 0)
+        for step in (steps_d - 2, steps_d - 1):
+            pair_copy(step).wait_send()
+
+    def to_plus(src, dst, recv, send, block):
+        return remote(src.at[block], dst.at[block], send.at[block], recv.at[block], plus, 0)
+
+    def to_minus(src, dst, recv, send, block):
+        return remote(src.at[block], dst.at[block], send.at[block], recv.at[block], minus, 0)
+
+    def even_odd(block, even, odd):
+        @pl.when(lax.rem(block, 2) == 0)
+        def _():
+            even()
+
+        @pl.when(lax.rem(block, 2) == 1)
+        def _():
+            odd()
+
+    def near_even(block):
+        return to_minus(agg.at[minus], two_minus, minus_recv, near_send, block)
+
+    def near_odd(block):
+        return to_plus(agg.at[plus], two_plus, plus_recv, near_send, block)
+
+    def far_even(block):
+        return to_plus(agg.at[far], one_in, one_recv, one_send, block)
+
+    def far_odd(block):
+        return to_minus(agg.at[far], one_in, one_recv, one_send, block)
+
+    def last_even(block):
+        return to_plus(agg.at[plus], two_plus, plus_recv, two_send, block)
+
+    def last_odd(block):
+        return to_minus(agg.at[minus], two_minus, minus_recv, two_send, block)
+
+    first = (plus, minus)
+    u_copy(5).wait_recv()
+    u_copy(3).wait_recv()
+    pick([(plus, 0), (minus, 0), (plus, 1), (minus, 1)])
+    gate_up(picked, expert_in, expert_out)
+    u_copy(4).wait_recv()
+    u_copy(7).start()
+    u_copy(6).wait_recv()
+    u_copy(8).start()
+    down([(plus, 0), (minus, 0), (plus, 1), (minus, 1)], first, expert_in,
+         lambda block: even_odd(block, lambda: near_even(block).start(), lambda: near_odd(block).start()))
+    pl.semaphore_signal(credit, inc=1, device_id={'ep': peer(0, 1)}, device_id_type=MESH)
+
+    second = (far, 0)
+    for k in (0, 7, 8):
+        u_copy(k).wait_recv()
+    pick([(far, 0), (0, 0), (far, 1), (0, 1)])
+    gate_up(picked, expert_in, expert_out)
+    pl.semaphore_wait(credit, 1)
+    down([(far, 0), (0, 0), (far, 1), (0, 1)], second, None,
+         lambda block: even_odd(block, lambda: far_even(block).start(), lambda: far_odd(block).start()))
+
+    def relay_body(block, carry):
+        def even():
+            far_even(block).wait_recv()
+            agg[plus, block] = agg[plus, block] + one_in[block]
+            last_even(block).start()
+
+        def odd():
+            far_odd(block).wait_recv()
+            agg[minus, block] = agg[minus, block] + one_in[block]
+            last_odd(block).start()
+
+        even_odd(block, even, odd)
+        return carry
+
+    lax.fori_loop(0, steps_d, relay_body, 0)
+
+    def final_body(block, carry):
+        last_even(block).wait_recv()
+        last_odd(block).wait_recv()
+        at = pl.ds(pl.multiple_of(block * D_TILE, D_TILE), D_TILE)
+        routed = agg[0, block] + two_plus[block] + two_minus[block]
+        out_ref[:, at] = (mid_ref[:, at].astype(jnp.float32) + routed + shared[:, at].astype(jnp.float32)).astype(jnp.bfloat16)
+
+        def even():
+            near_even(block).wait_send()
+            far_even(block).wait_send()
+            last_even(block).wait_send()
+
+        def odd():
+            near_odd(block).wait_send()
+            far_odd(block).wait_send()
+            last_odd(block).wait_send()
+
+        even_odd(block, even, odd)
+        return carry
+
+    lax.fori_loop(0, steps_d, final_body, 0)
+    for k in range(len(peers)):
+        table_copy(k).wait_send()
+    for k in range(len(routes)):
+        u_copy(k).wait_send()
+
+
+def moe_block(u_norm, x_mid, table, w_gate, w_up, w_down, shared_gate, shared_up, shared_down, ep_size, capacity):
+    tokens, width = u_norm.shape
+    local, _, ff = w_gate.shape
+    chips = ep_size // CORES
+    blocks = width // D_TILE
+    rows = CORES * 2 * capacity
+    f32, bf16 = jnp.float32, jnp.bfloat16
+    dma = pltpu.SemaphoreType.DMA
+    vmem = pl.BlockSpec(memory_space=pltpu.VMEM)
+    hbm = pl.BlockSpec(memory_space=pl.ANY)
+    return pl.pallas_call(
+        functools.partial(moe_kernel, chips, capacity),
+        out_shape=jax.ShapeDtypeStruct((tokens, width), bf16),
+        in_specs=[vmem] * 3 + [hbm] * 6,
+        out_specs=vmem,
+        scratch_shapes=[
+            pltpu.VMEM((ep_size - 1, tokens, width), bf16),
+            pltpu.VMEM((rows, width), bf16),
+            pltpu.VMEM((local, rows, ff), bf16),
+            pltpu.VMEM((2, local, width, F_TILE), bf16),
+            pltpu.VMEM((local, rows, D_TILE), bf16),
+            pltpu.VMEM((chips, blocks, tokens, D_TILE), f32),
+            pltpu.VMEM((2, 2, tokens, D_TILE), f32),
+            pltpu.VMEM((blocks, 2, tokens, D_TILE), f32),
+            pltpu.VMEM((blocks, tokens, D_TILE), f32),
+            pltpu.VMEM((blocks, tokens, D_TILE), f32),
+            pltpu.VMEM((blocks, tokens, D_TILE), f32),
+            pltpu.VMEM((ep_size,) + table.shape, f32),
+            pltpu.VMEM((ep_size, local, tokens, tokens), f32),
+            pltpu.VMEM((ep_size, tokens, capacity), bf16),
+            pltpu.VMEM((tokens, width), bf16),
+            dma((2, 2 * local)),
+            dma((ep_size - 1,)), dma((ep_size,)),
+            dma((9,)), dma((9,)),
+            dma((2,)), dma((blocks,)),
+            dma((blocks,)), dma((blocks,)), dma((blocks,)), dma((blocks,)), dma((blocks,)), dma((blocks,)),
+            pltpu.SemaphoreType.REGULAR,
+        ],
+        compiler_params=pltpu.CompilerParams(collective_id=0, has_side_effects=True, vmem_limit_bytes=67043328),
+        name='moe',
+    )(u_norm, x_mid, table, w_gate, w_up, w_down, shared_gate, shared_up, shared_down)
 
 
 def solution(mesh):
@@ -99,20 +457,10 @@
     def local_step(hidden, positions, ckv_cache, kpe_cache, topk_ids, attn_gain, w_dq, q_gain, w_uq, w_dkv, kv_gain, w_uk, w_uv, w_out, ffn_gain, w_router, w_gate, w_up, w_down, shared_gate, shared_up, shared_down):
         x_mid, c_new, k_new = attention_block(hidden, positions, ckv_cache, kpe_cache, attn_gain, w_dq, q_gain, w_uq, w_dkv, kv_gain, w_uk, w_uv, w_out)
         u_norm = rms_norm(x_mid, ffn_gain).astype(jnp.bfloat16)
-        tokens, width = u_norm.shape
         experts = w_router.shape[1]
-        local = w_gate.shape[0]
-        capacity = (CAP_FACTOR * tokens * topk_ids.shape[1] + experts - 1) // experts
-        weights, slots = route_weights(u_norm, topk_ids, w_router, capacity)
-        route_mat = jnp.any(slots[:, :, None] == jnp.arange(experts * capacity)[None, None, :], axis=1).astype(jnp.bfloat16)
-        outgoing = jnp.einsum('tm,td->md', route_mat, u_norm, preferred_element_type=jnp.float32).astype(jnp.bfloat16)
-        incoming = lax.all_to_all(outgoing, 'ep', 0, 0, tiled=True).reshape(ep_size, local, capacity, width)
-        results = expert_block(incoming, w_gate, w_up, w_down).reshape(ep_size * local * capacity, width)
-        returned = lax.all_to_all(results, 'ep', 0, 0, tiled=True)
-        picked = jnp.take(returned, jnp.maximum(slots, 0), axis=0)
-        routed = jnp.sum(weights[:, :, None] * picked.astype(jnp.float32), axis=1)
-        shared_out = shared_block(u_norm, shared_gate, shared_up, shared_down)
-        hidden_out = (x_mid.astype(jnp.float32) + routed + shared_out.astype(jnp.float32)).astype(jnp.bfloat16)
+        capacity = (CAP_FACTOR * topk_ids.size + experts - 1) // experts
+        table = route_table(u_norm, topk_ids, w_router, w_gate.shape[0], capacity)
+        hidden_out = moe_block(u_norm, x_mid, table, w_gate, w_up, w_down, shared_gate, shared_up, shared_down, ep_size, capacity)
         return hidden_out, c_new, k_new
 
     in_specs = (batch,) * 5 + (whole,) * 11 + (by_expert,) * 3 + (whole,) * 3

time: 653 us -> 301 us (0.46); the launches traced: 646 us -> 301 us
  Pallas kernels: 0 us -> 207 us
  blocking collectives: 179 us -> 0 us
  matrix products: 216 us -> 68.5 us
  waiting for transfers between devices: 147 us -> 0 us
  local copies, waits for them, and re-layouts: 73.5 us -> 15.7 us
  other arithmetic: 23 us -> 7.99 us
    pallas_call x0 -> x1, Pallas kernels: none -> 207 us  [moe_block(): pl.pallas_call(functools.partial(moe_kernel, chips, capacity), out_shape=...]
    all_to_all x1 -> x0, blocking collectives: 179 us -> none  [local_step(): lax.all_to_all(outgoing, 'ep', 0, 0, tiled=True)]
    dot_general x7 -> x2, matrix products: 153 us -> 0.61 us  [the longest x1 0.47 us: route_table(): jnp.dot(u_norm, w_router, preferred_element_type=jnp.float32)]
    all_to_all x1 -> x0, waiting for transfers between devices: 147 us -> none  [local_step(): returned = lax.all_to_all(results, 'ep', 0, 0, tiled=True)]
    gather x7 -> x0, local copies, waits for them, and re-layouts: 41.1 us -> none  [the longest x2 35.5 us: local_step(): picked = jnp.take(returned, jnp.maximum(slots, 0), axis=0)]
    convert_element_type x1 -> x0, local copies, waits for them, and re-layouts: 13.2 us -> none  [expert_block(): jnp.einsum('slcf,lfd->slcd', act, w_down, preferred_element_type=jnp.floa...]
    reduce_sum x4 -> x0, other arithmetic: 12.3 us -> none  [the longest x1 12.2 us: local_step(): routed = jnp.sum(weights[:, :, None] * picked.astype(jnp.float32), axis=1)]
  transfers between devices with their start and end apart: 1 -> 0, of which waited for: 1 -> 0; matrix products, arithmetic and copies ran while one was open for 4% -> 0% of each run, Pallas kernels for 0% -> 0%
where the time goes in v1:
time: 301 us
  Pallas kernels  207 us (69%)
  matrix products  68.5 us (23%)
  local copies, waits for them, and re-layouts  15.7 us (5%)
  other arithmetic  7.99 us (3%)
    pallas_call x1, Pallas kernels, moe_block(): pl.pallas_call(functools.partial(moe_kernel, chips, capacity), out_shape=...  207 us
    dot_general x1, matrix products, attention_block(): jnp.einsum('thc,tsc->ths', q_abs, ckv_cache, preferred_element_type=jnp.f...  15.2 us
    dot_general x1, matrix products, attention_block(): jnp.einsum('ths,tsc->thc', p_cache, ckv_cache, preferred_element_type=jnp...  14.5 us
    dot_general x1, matrix products, attention_block(): jnp.dot(heads_out.reshape(tokens, heads * VALUE_DIM), w_out, preferred_el...  10.4 us
    dot_general x1, matrix products, attention_block(): jnp.dot(normed, w_dq, preferred_element_type=jnp.float32)  7.95 us
    unnamed x51, local copies, waits for them, and re-layouts  7.15 us

profile of v1, /device:TPU:112, one launch (start us, length us, event | category | flops | bytes accessed | tf_op | source)
XLA Modules:
  0.0 300.7 jit_solution(992334065770089601)
XLA Ops:
  0.6 0.7 convert_element_type.89
  1.3 1.6 fusion.4
  3.0 0.0 slice-start
  3.0 5.0 %fusion.30 = f32[128,576]{0,1:T(8,128)S(1)} fusion(bf16[5120,576]{0,1:T(8,128)(2,1)} %param.31, bf16[128,5120]{1,0:T(8,128)(2,1)} %param.22, f32[5120]{0:T(1024)S(1)} %convert_element_type.89, f32[128]{0:T(128)S(1)} %add_rsqrt_fusion.3), kind=kOutput, calls=%fused_computation.43 | convolution fusion | flops 757596160 | bytes 7524864 | tf_op jit(solution)/shard_map/dot_general | solution.py:51
  8.1 0.1 subtract_convert_fusion.1
  8.2 0.1 copy.52
  8.3 0.4 copy-done.7
  8.7 0.1 copy.53
  8.9 0.0 copy-start.16
  8.9 0.0 slice-start.1
  8.9 7.9 %multiply_reduce_fusion = (f32[128]{0:T(128)S(1)}, f32[128,1536]{1,0:T(8,128)S(1)}) fusion(bf16[5120,1536]{1,0:T(8,128)(2,1)} %param.28, bf16[128,5120]{1,0:T(8,128)(2,1)S(1)} %copy-done, f32[5120]{0:T(1024)S(1)} %convert_element_type.89, f32[128]{0:T(128)S(1)} %add_rsqrt_fusion.3), kind=kOutput, calls=%fused_computation.38 | convolution fusion | flops 2016280448 | bytes 17847296 | tf_op jit(solution)/shard_map/dot_general | solution.py:47
  16.9 2.4 convolution_convert_fusion
  19.3 1.5 copy.47
  20.8 0.4 copy.64
  21.2 0.1 convert_element_type.96
  21.3 0.5 subtract_convert_fusion
  21.9 0.0 copy-start.5
  21.9 0.1 copy.60
  22.1 0.5 fusion.34
  22.5 2.4 convert_bitcast_fusion
  24.9 0.0 copy-start.20
  24.9 15.2 %fusion.17 = f32[128,16,256]{2,1,0:T(8,128)S(1)} fusion(bf16[128,256,512]{2,1,0:T(8,128)(2,1)} %param.24, bf16[128,16,512]{2,0,1:T(8,128)(2,1)S(1)} %convert_bitcast_fusion), kind=kOutput, calls=%fused_computation.26 | convolution fusion | flops 536870912 | bytes 37748736 | tf_op jit(solution)/shard_map/thc,tsc->ths/dot_general | solution.py:56
  40.1 0.0 copy-done.3
  40.2 0.1 iota_compare_fusion
  40.3 0.0 copy-start.18
  40.3 3.6 %fusion.42 = (f32[128,16]{1,0:T(8,128)S(1)}, f32[128,16,256]{2,1,0:T(8,128)S(1)}) fusion(f32[128,16,256]{2,1,0:T(8,128)S(1)} %fusion.17, bf16[128,256,64]{1,2,0:T(8,128)(2,1)} %param.25, bf16[128,16,32]{2,1,0:T(8,128)(2,1)} %copy-done.5, bf16[128,16,32]{2,1,0:T(8,128)(2,1)} %copy-done.4, pred[128,256]{1,0:T(8,128)(4,1)S(1)} %iota_compare_fusion), kind=kOutput, calls=%fused_computation.75 | convolution fusion | flops 69728256 | bytes 8691712 | tf_op jit(solution)/shard_map/thr,tsr->ths/dot_general | solution.py:56
  43.9 0.1 multiply_reduce_fusion.1
  44.0 0.8 fusion.58
  44.8 1.8 copy.58
  46.6 3.0 fusion.15
  49.6 0.7 fusion.14
  50.2 0.7 fusion.41
  50.9 0.1 multiply_convert_fusion.2
  51.1 0.8 copy.54
  51.9 14.5 %add_convert_fusion = bf16[128,16,512]{2,1,0:T(8,128)(2,1)} fusion(f32[128,512]{1,0:T(8,128)} %copy.54, f32[128,16]{1,0:T(8,128)} %get-tuple-element.17, bf16[128,256,512]{2,1,0:T(8,128)(2,1)} %param.24, f32[128,16,256]{2,1,0:T(8,128)S(1)} %get-tuple-element.23, f32[128,16]{1,0:T(8,128)} %get-tuple-element.16, f32[128,16]{1,0:T(8,128)} %copy-done.11), kind=kOutput, calls=%fused_computation.2 | convolution fusion | flops 541589504 | bytes 38035456 | tf_op jit(solution)/shard_map/ths,tsc->thc/dot_general | solution.py:66
  66.4 4.1 %copy.62 = bf16[512,2048]{0,1:T(8,128)(2,1)} copy(bf16[512,2048]{1,0:T(8,128)(2,1)} %param.34) | data formatting | bytes 4194304 | tf_op jit(solution)/shard_map/reshape | solution.py:67
  70.5 3.1 %fusion.19 = bf16[16,128,128]{1,2,0:T(8,128)(2,1)S(1)} fusion(bf16[512,16,128]{0,2,1:T(8,128)(2,1)} %bitcast.44, bf16[128,16,512]{2,1,0:T(8,128)(2,1)S(1)} %copy-done.6), kind=kOutput, calls=%fused_computation.28 | convolution fusion | flops 268697600 | bytes 4718592 | tf_op jit(solution)/shard_map/thc,chv->thv/dot_general | solution.py:67
  73.6 10.4 %fusion.1 = (f32[128]{0:T(128)S(1)}, bf16[128,5120]{1,0:T(8,128)(2,1)S(1)}) fusion(bf16[128,2048]{0,1:T(8,128)(2,1)S(1)} %bitcast.45, bf16[2048,5120]{1,0:T(8,128)(2,1)} %param.35, bf16[128,5120]{1,0:T(8,128)(2,1)S(1)} %copy-done), kind=kOutput, calls=%fused_computation.8 | convolution fusion | flops 2688286720 | bytes 24117760 | tf_op jit(solution)/shard_map/dot_general | solution.py:68
  84.1 1.0 copy-done.1
  85.1 0.4 fusion.3.u_ref
  85.5 1.0 copy-done.2
  86.6 0.5 select_reduce_fusion
  87.1 0.1 and_select_fusion
  87.2 0.6 maximum_bitcast_fusion.table_ref
  87.9 207.4 %moe.1 = bf16[128,5120]{1,0:T(8,128)(2,1)} custom-call(bf16[128,5120]{1,0:T(8,128)(2,1)} %copy-done.2, bf16[128,5120]{1,0:T(8,128)(2,1)} %copy-done.1, f32[24,128]{1,0:T(8,128)} %maximum_bitcast_fusion.table_ref, bf16[2,5120,1536]{2,1,0:T(8,128)(2,1)} %gate_ref.1, bf16[2,5120,1536]{2,1,0:T(8,128)(2,1)} %up_ref.1, bf16[2,1536,5120]{2,1,0:T(8,128)(2,1)} %down_ref.1, ...), custom_call_target="tpu_custom_call" | custom-call | tf_op jit(solution)/shard_map/moe/pallas_call | solution.py:418
  295.2 1.3 pad_maximum_fusion.3
  296.5 1.7 copy.57
  298.2 2.5 copy.81
  (54 shorter events, 0.2 us)
Async XLA Ops:
  3.0 5.0 %copy-start.19 = (s32[128]{0:T(128)S(1)}, s32[128]{0:T(128)}, u32[]{:S(2)}) copy-start(s32[128]{0:T(128)} %param.23) | copy-start | bytes 1540
  3.0 5.8 %copy-start = (bf16[128,5120]{1,0:T(8,128)(2,1)S(1)}, bf16[128,5120]{1,0:T(8,128)(2,1)}, u32[]{:S(2)}) copy-start(bf16[128,5120]{1,0:T(8,128)(2,1)} %param.22) | copy-start | bytes 3932164
  3.0 13.8 %slice-start = ((s8[9437184]{0:T(1024)(128)(4,1)}), s8[1048576]{0:T(1024)(128)(4,1)S(1)}, s32[]{:S(2)}) async-start(s8[9437184]{0:T(1024)(128)(4,1)} %bitcast.40), calls=%async_computation | async-start | bytes 2097152
  8.0 0.7 copy-start.7
  8.2 13.7 %copy-start.13 = (bf16[128,32]{0,1:T(8,128)(2,1)}, bf16[128,32]{0,1:T(8,128)(2,1)S(1)}, u32[]{:S(2)}) copy-start(bf16[128,32]{0,1:T(8,128)(2,1)S(1)} %get-tuple-element.14) | copy-start | bytes 24580
  8.2 13.7 %copy-start.14 = (bf16[128,32]{0,1:T(8,128)(2,1)}, bf16[128,32]{0,1:T(8,128)(2,1)S(1)}, u32[]{:S(2)}) copy-start(bf16[128,32]{0,1:T(8,128)(2,1)S(1)} %get-tuple-element.15) | copy-start | bytes 24580
  8.9 8.0 %copy-start.16 = (bf16[1536]{0:T(1024)(128)(2,1)S(1)}, bf16[1536]{0:T(1024)(128)(2,1)}, u32[]{:S(2)}) copy-start(bf16[1536]{0:T(1024)(128)(2,1)} %param.29) | copy-start | bytes 9220
  8.9 8.0 %slice-start.1 = ((s8[9437184]{0:T(1024)(128)(4,1)}), s8[4194304]{0:T(1024)(128)(4,1)S(1)}, s32[]{:S(2)}) async-start(s8[9437184]{0:T(1024)(128)(4,1)} %bitcast.40), calls=%async_computation.1 | async-start | bytes 8388608
  8.9 8.0 %slice-start.2 = ((s8[9437184]{0:T(1024)(128)(4,1)}), s8[4194304]{0:T(1024)(128)(4,1)S(1)}, s32[]{:S(2)}) async-start(s8[9437184]{0:T(1024)(128)(4,1)} %bitcast.40), calls=%async_computation.2 | async-start | bytes 8388608
  21.9 3.0 copy-start.4
  21.9 3.0 copy-start.5
  24.9 15.2 %copy-start.3 = (bf16[128,16,512]{2,0,1:T(8,128)(2,1)}, bf16[128,16,512]{2,0,1:T(8,128)(2,1)S(1)}, u32[]{:S(2)}) copy-start(bf16[128,16,512]{2,0,1:T(8,128)(2,1)S(1)} %convert_bitcast_fusion) | copy-start | bytes 6291460
  24.9 15.2 %copy-start.20 = (s32[128]{0:T(128)S(1)}, s32[128]{0:T(128)}, u32[]{:S(2)}) copy-start(s32[128]{0:T(128)} %param.23) | copy-start | bytes 1540
  40.2 3.6 %copy-start.8 = (f32[128,576]{0,1:T(8,128)S(1)}, f32[128,576]{0,1:T(8,128)}, u32[]{:S(2)}) copy-start(f32[128,576]{0,1:T(8,128)} %copy-done.7) | copy-start | bytes 884740
  40.3 3.7 %copy-start.18 = (bf16[512]{0:T(512)(128)(2,1)S(1)}, bf16[512]{0:T(512)(128)(2,1)}, u32[]{:S(2)}) copy-start(bf16[512]{0:T(512)(128)(2,1)} %param.32) | copy-start | bytes 3076
  49.5 1.4 copy-start.9
  49.6 1.4 copy-start.11
  51.1 15.4 %copy-start.10 = (bf16[128,512]{0,1:T(8,128)(2,1)}, bf16[128,512]{0,1:T(8,128)(2,1)S(1)}, u32[]{:S(2)}) copy-start(bf16[128,512]{0,1:T(8,128)(2,1)S(1)} %multiply_convert_fusion.2) | copy-start | bytes 393220
  66.4 4.1 %copy-start.6 = (bf16[128,16,512]{2,1,0:T(8,128)(2,1)S(1)}, bf16[128,16,512]{2,1,0:T(8,128)(2,1)}, u32[]{:S(2)}) copy-start(bf16[128,16,512]{2,1,0:T(8,128)(2,1)} %add_convert_fusion) | copy-start | bytes 6291460
  73.6 10.5 %copy-start.15 = (bf16[5120]{0:T(1024)(128)(2,1)S(1)}, bf16[5120]{0:T(1024)(128)(2,1)}, u32[]{:S(2)}) copy-start(bf16[5120]{0:T(1024)(128)(2,1)} %param.36) | copy-start | bytes 30724
  84.0 1.1 copy-start.1
  84.0 1.5 copy-start.17
  84.1 2.5 copy-start.12
  85.5 1.1 copy-start.2

commit v2 on v1

v2 whole, which is shorter than its diff:
```python
import functools

import jax
import jax.numpy as jnp
from jax import lax
from jax.experimental import pallas as pl
from jax.experimental.pallas import tpu as pltpu
from jax.sharding import PartitionSpec as P

NOPE_DIM = 128
ROPE_DIM = 64
VALUE_DIM = 128
QK_DIM = NOPE_DIM + ROPE_DIM
EPSILON = 1e-6
ROUTE_SCALE = 2.5
ROPE_BASE = 10000.0
CAP_FACTOR = 2
CORES = 2
F_TILE = 256
D_TILE = 512
W_SLOTS = 3
S_SLOTS = 3
P_TILE = 1024
SEQS = 8
PARTS = 2
MESH = pl.DeviceIdType.MESH


def rms_norm(vec, gain):
    vec = vec.astype(jnp.float32)
    scale = lax.rsqrt(jnp.mean(vec * vec, axis=-1, keepdims=True) + EPSILON)
    return vec * scale * gain.astype(jnp.float32)


def rotary(vec, positions):
    half = ROPE_DIM // 2
    freqs = ROPE_BASE ** (-jnp.arange(half).astype(jnp.float32) / half)
    angle = positions.astype(jnp.float32)[..., None] * freqs
    cosine = jnp.cos(angle)
    sine = jnp.sin(angle)
    first = vec[..., :half]
    second = vec[..., half:]
    return jnp.concatenate([first * cosine - second * sine, first * sine + second * cosine], axis=-1)


def attend_kernel(heads, position_ref, q_abs_ref, q_rot_ref, ckv_ref, kpe_ref, c_new_ref, k_new_ref, context_ref, raw):
    _, cache_len, kv_rank = ckv_ref.shape
    f32, bf16 = jnp.float32, jnp.bfloat16
    rows = heads * SEQS
    wide = q_rot_ref.shape[2]
    pair = wide // ROPE_DIM
    scale = QK_DIM ** -0.5

    def per_row(block):
        return jnp.concatenate([block] * heads, axis=0)

    row_seq = lax.broadcasted_iota(jnp.int32, (rows, 1), 0) % SEQS
    for part in range(PARTS):
        seqs = pl.ds(part * SEQS, SEQS)
        q_abs = q_abs_ref[:, seqs, :].reshape(rows, kv_rank)
        q_rot = q_rot_ref[:, seqs, :].reshape(rows, wide)
        ckv = ckv_ref[seqs].reshape(SEQS * cache_len, kv_rank)
        raw[part] = lax.dot_general(ckv, q_abs, (((1,), (1,)), ((), ())), preferred_element_type=f32)
        lane_seq = lax.broadcasted_iota(jnp.int32, (cache_len, rows), 1) % SEQS
        scores = raw[part, pl.ds(0, cache_len)]
        for g in range(1, SEQS):
            scores = jnp.where(lane_seq == g, raw[part, pl.ds(g * cache_len, cache_len)], scores)
        lane_part = lax.broadcasted_iota(jnp.int32, (rows, wide), 1) // ROPE_DIM
        spread = jnp.concatenate([jnp.where(row_seq == g + lane_part, q_rot.astype(f32), 0.0) for g in range(0, SEQS, pair)], axis=1).astype(bf16)
        rope = jnp.dot(spread, kpe_ref[seqs].reshape(SEQS * ROPE_DIM, cache_len), preferred_element_type=f32)
        scores = (scores.T + rope) * scale
        place = lax.broadcasted_iota(jnp.int32, (SEQS, cache_len), 1)
        scores = jnp.where(per_row(place) < per_row(jnp.broadcast_to(position_ref[seqs], (SEQS, cache_len))), scores, -1e30)
        c_new = per_row(c_new_ref[seqs].astype(f32))
        own = jnp.sum(q_abs.astype(f32) * c_new, axis=1, keepdims=True) + jnp.sum(jnp.where(lane_part == 0, q_rot.astype(f32) * per_row(k_new_ref[seqs].astype(f32)), 0.0), axis=1, keepdims=True)
        own = own * scale
        peak = jnp.maximum(jnp.max(scores, axis=1, keepdims=True), own)
        e_cache = jnp.exp(scores - peak)
        e_own = jnp.exp(own - peak)
        denominator = jnp.sum(e_cache, axis=1, keepdims=True) + e_own
        p_cache = e_cache / denominator
        p_own = (e_own / denominator).astype(bf16).astype(f32)
        probs = jnp.concatenate([jnp.where(row_seq == g, p_cache, 0.0).astype(bf16) for g in range(SEQS)], axis=1)
        context = jnp.dot(probs, ckv, preferred_element_type=f32) + p_own * c_new
        context_ref[:, seqs, :] = context.astype(bf16).reshape(heads, SEQS, kv_rank)


def attend(q_abs, q_rot, ckv_cache, kpe_cache, c_new, k_new, positions):
    heads, tokens, kv_rank = q_abs.shape
    cache_len = ckv_cache.shape[1]
    step = SEQS * PARTS
    doubled = jnp.concatenate([q_rot, q_rot], axis=2)
    k_doubled = jnp.concatenate([k_new, k_new], axis=1)
    wide = doubled.shape[2]
    by_head = lambda i: (0, i, 0)
    by_seq = lambda i: (i, 0, 0)
    return pl.pallas_call(
        functools.partial(attend_kernel, heads),
        grid=(tokens // step,),
        out_shape=jax.ShapeDtypeStruct((heads, tokens, kv_rank), jnp.bfloat16),
        in_specs=[
            pl.BlockSpec((step, 1), lambda i: (i, 0)),
            pl.BlockSpec((heads, step, kv_rank), by_head),
            pl.BlockSpec((heads, step, wide), by_head),
            pl.BlockSpec((step, cache_len, kv_rank), by_seq),
            pl.BlockSpec((step, ROPE_DIM, cache_len), by_seq),
            pl.BlockSpec((step, kv_rank), lambda i: (i, 0)),
            pl.BlockSpec((step, wide), lambda i: (i, 0)),
        ],
        out_specs=pl.BlockSpec((heads, step, kv_rank), by_head),
        scratch_shapes=[pltpu.VMEM((PARTS, SEQS * cache_len, heads * SEQS), jnp.float32)],
        compiler_params=pltpu.CompilerParams(dimension_semantics=('arbitrary',), vmem_limit_bytes=40 * 2**20),
        name='attend',
    )(positions[:, None], q_abs, doubled, ckv_cache, jnp.swapaxes(kpe_cache, 1, 2), c_new, k_doubled)


def attention_block(hidden, positions, ckv_cache, kpe_cache, attn_gain, w_dq, q_gain, w_uq, w_dkv, kv_gain, w_uk, w_uv, w_out):
    tokens = hidden.shape[0]
    kv_rank = w_uk.shape[0]
    heads = w_uk.shape[1] // NOPE_DIM
    normed = rms_norm(hidden, attn_gain).astype(jnp.bfloat16)
    c_q = rms_norm(jnp.dot(normed, w_dq, preferred_element_type=jnp.float32), q_gain).astype(jnp.bfloat16)
    query = jnp.dot(c_q, w_uq, preferred_element_type=jnp.float32).astype(jnp.bfloat16).reshape(tokens, heads, QK_DIM)
    q_nope = query[:, :, :NOPE_DIM]
    q_rot = rotary(query[:, :, NOPE_DIM:].astype(jnp.float32), positions[:, None]).astype(jnp.bfloat16)
    kv_proj = jnp.dot(normed, w_dkv, preferred_element_type=jnp.float32)
    c_new = rms_norm(kv_proj[:, :kv_rank], kv_gain).astype(jnp.bfloat16)
    k_new = rotary(kv_proj[:, kv_rank:], positions).astype(jnp.bfloat16)
    q_abs = jnp.einsum('thn,chn->htc', q_nope, w_uk.reshape(kv_rank, heads, NOPE_DIM), preferred_element_type=jnp.float32).astype(jnp.bfloat16)
    context = attend(q_abs, jnp.swapaxes(q_rot, 0, 1), ckv_cache, kpe_cache, c_new, k_new, positions)
    heads_out = jnp.einsum('htc,chv->thv', context, w_uv.reshape(kv_rank, heads, VALUE_DIM), preferred_element_type=jnp.float32).astype(jnp.bfloat16)
    attn_out = jnp.dot(heads_out.reshape(tokens, heads * VALUE_DIM), w_out, preferred_element_type=jnp.float32)
    x_mid = (hidden.astype(jnp.float32) + attn_out).astype(jnp.bfloat16)
    return x_mid, c_new, k_new


def route_table(u_norm, topk_ids, w_router, local, capacity):
    tokens = u_norm.shape[0]
    experts = w_router.shape[1]
    gates = jax.nn.sigmoid(jnp.dot(u_norm, w_router, preferred_element_type=jnp.float32))
    hits = jnp.any(topk_ids[:, :, None] == jnp.arange(experts), axis=1)
    total = jnp.sum(jnp.where(hits, gates, 0.0), axis=1, keepdims=True)
    group_hits = hits[:, ::local]
    earlier = (jnp.arange(tokens)[:, None] > jnp.arange(tokens)[None, :]).astype(jnp.bfloat16)
    rank = jnp.dot(earlier, group_hits.astype(jnp.bfloat16), preferred_element_type=jnp.float32)
    slots = jnp.where(group_hits & (rank < capacity), rank, -1.0)
    weights = jnp.where(hits, ROUTE_SCALE * gates / total, 0.0)
    table = jnp.concatenate([weights, slots], axis=1).T
    return jnp.pad(table, ((0, -table.shape[0] % 8), (0, 0)))


def moe_kernel(chips, capacity, u_ref, mid_ref, table_ref, gate_ref, up_ref, down_ref, sgate_ref, sup_ref, sdown_ref, out_ref,
               far_u, picked, act, sact, wbuf, eout, agg, stage, landed, one_in, two_plus, two_minus, tables, scales, spread,
               w_sem, table_send, table_recv, u_send, u_recv, pair_send, pair_recv, near_send, one_send, one_recv, two_send, plus_recv, minus_recv, credit):
    tokens, width = u_ref.shape
    local, _, ff = gate_ref.shape
    experts = local * chips * CORES
    half = tokens // 2
    f_blocks = ff // F_TILE
    steps_f = local * f_blocks
    steps_d = width // D_TILE
    cols = D_TILE // F_TILE
    me = lax.axis_index('ep')
    chip = lax.div(me, CORES)
    core = lax.rem(me, CORES)

    def peer(offset, other):
        return lax.rem(chip + offset, chips) * CORES + (1 - core if other else core)

    def remote(src, dst, send_sem, recv_sem, offset, other):
        return pltpu.make_async_remote_copy(src_ref=src, dst_ref=dst, send_sem=send_sem, recv_sem=recv_sem, device_id={'ep': peer(offset, other)}, device_id_type=MESH)

    plus, minus, far = 1, chips - 1, chips // 2
    peers = [(o, q) for q in range(CORES) for o in range(chips) if (o, q) != (0, 0)]

    def u_at(offset, other):
        index = other * chips + offset
        return u_ref if index == 0 else far_u.at[index - 1]

    def expert_in(step, slot):
        e, b = lax.div(step, f_blocks), lax.rem(step, f_blocks)
        at = pl.ds(pl.multiple_of(b * F_TILE, F_TILE), F_TILE)
        return [pltpu.make_async_copy(ref.at[e, :, at], wbuf.at[slot, k], w_sem.at[slot, k]) for k, ref in enumerate((gate_ref, up_ref))]

    def shared_in(step, slot):
        at = pl.ds(pl.multiple_of(step * F_TILE, F_TILE), F_TILE)
        return [pltpu.make_async_copy(ref.at[:, at], wbuf.at[slot, k], w_sem.at[slot, k]) for k, ref in enumerate((sgate_ref, sup_ref))]

    def down_copies(piece, step, slot):
        copies = []
        for e in range(local):
            for h in range(cols):
                at = pl.ds(pl.multiple_of(step * D_TILE + h * F_TILE, F_TILE), F_TILE)
                copies.append(pltpu.make_async_copy(piece(e, at), wbuf.at[slot, e, pl.ds(h * ff, ff)], w_sem.at[slot, e * cols + h]))
        return copies

    def expert_out(step, slot):
        return down_copies(lambda e, at: down_ref.at[e, :, at], step, slot)

    def shared_down(step, slot):
        return down_copies(lambda e, at: sdown_ref.at[pl.ds(e * ff, ff), at], step, slot)

    def begin(copies):
        for copy in copies:
            copy.start()

    def finish(copies):
        for copy in copies:
            copy.wait()

    ahead = W_SLOTS - 1

    def start(count, load, base):
        for step in range(count):
            begin(load(step, (base + step) % W_SLOTS))

    def stream(step, high, base, load, following):
        coming = step + ahead
        to = lax.rem(base + coming, W_SLOTS)

        @pl.when(coming < high)
        def _():
            begin(load(coming, to))

        if following is not None:
            @pl.when(coming >= high)
            def _():
                begin(following(coming - high, to))

        slot = lax.rem(base + step, W_SLOTS)
        finish(load(step, slot))
        return slot

    def gate_up(base, lhs, rows, into, load, following, hook):
        def body(step, carry):
            slot = stream(step, steps_f, base, load, following)
            e, b = lax.div(step, f_blocks), lax.rem(step, f_blocks)
            h_gate = jnp.dot(lhs[:rows], wbuf[slot, 0], preferred_element_type=jnp.float32)
            h_up = jnp.dot(lhs[:rows], wbuf[slot, 1], preferred_element_type=jnp.float32)
            into[e, pl.ds(0, rows), pl.ds(pl.multiple_of(b * F_TILE, F_TILE), F_TILE)] = (h_gate * jax.nn.sigmoid(h_gate) * h_up).astype(jnp.bfloat16)
            if hook is not None:
                hook(step)
            return carry

        lax.fori_loop(0, steps_f, body, 0)

    def shared_out(base, low, high, following):
        def body(step, carry):
            slot = stream(step, high, base - low, shared_down, following)
            for h in range(cols):
                total = None
                for e in range(local):
                    piece = jnp.dot(sact[e], wbuf[slot, e, pl.ds(h * ff, ff), :], preferred_element_type=jnp.float32)
                    total = piece if total is None else total + piece
                out_ref[:, pl.ds(pl.multiple_of(step * D_TILE + h * F_TILE, F_TILE), F_TILE)] = total.astype(jnp.bfloat16)
            return carry

        lax.fori_loop(low, high, body, 0)

    with jax.named_scope('enter'):
        start(ahead, shared_in, 0)
        barrier = pltpu.get_barrier_semaphore()
        for o, q in peers:
            pl.semaphore_signal(barrier, inc=1, device_id={'ep': peer(o, q)}, device_id_type=MESH)
        pl.semaphore_wait(barrier, len(peers))

    def table_copy(k):
        o, q = peers[k]
        back = q * chips + (chips - o) % chips
        return remote(table_ref, tables.at[back], table_send.at[k], table_recv.at[back], o, q)

    for k in range(len(peers)):
        table_copy(k).start()

    halves = pl.ds(0, half), pl.ds(half, half)
    routes = {
        'own': (u_at(0, 0), u_at(0, 1), 0, 1),
        'plus0': (u_at(0, 0).at[halves[0]], u_at(minus, 0).at[halves[0]], plus, 0),
        'plus1': (u_at(0, 0).at[halves[1]], u_at(minus, 0).at[halves[1]], plus, 0),
        'minus1': (u_at(0, 0).at[halves[1]], u_at(plus, 0).at[halves[1]], minus, 0),
        'minus0': (u_at(0, 0).at[halves[0]], u_at(plus, 0).at[halves[0]], minus, 0),
        'far0': (u_at(minus, 0).at[halves[0]], u_at(far, 0).at[halves[0]], plus, 0),
        'far1': (u_at(plus, 0).at[halves[1]], u_at(far, 0).at[halves[1]], minus, 0),
    }
    for name, offset in (('plus', minus), ('minus', plus), ('far', far)):
        for h in range(2):
            routes[f'{name}{h}_pair'] = (u_at(offset, 0).at[halves[h]], u_at(offset, 1).at[halves[h]], 0, 1)
    order = list(routes)

    def u_copy(name):
        src, dst, o, q = routes[name]
        k = order.index(name)
        return remote(src, dst, u_send.at[k], u_recv.at[k], o, q)

    def forward(name, *onward):
        u_copy(name).wait_recv()
        for one in onward:
            u_copy(one).start()

    def at_step(step, when, action):
        @pl.when(step == when)
        def _():
            action()

    for name in ('plus0', 'minus1', 'plus1', 'minus0', 'own'):
        u_copy(name).start()

    def first_halves():
        forward('plus0', 'far0', 'plus0_pair')
        forward('minus1', 'far1', 'minus1_pair')

    with jax.named_scope('shared_in'):
        gate_up(0, u_ref, tokens, sact, shared_in, shared_down, lambda step: at_step(step, steps_f * 3 // 4, first_halves))
    early = steps_d // 2
    near_base = steps_f + early
    far_base = near_base + steps_f + steps_d
    own_base = far_base + steps_f + steps_d
    rest_base = own_base + steps_f + steps_d
    with jax.named_scope('shared_out'):
        shared_out(steps_f, 0, early, expert_in)

    def place_tables(index, i):
        slot_row = tables[index, pl.ds(experts + me, 1), :]
        slot_col = jnp.transpose(jnp.broadcast_to(slot_row, (tokens, tokens)))
        lane = lax.broadcasted_iota(jnp.int32, (tokens, tokens), 1).astype(jnp.float32)
        spread[i] = jnp.where(slot_col == lane, 1.0, 0.0).astype(jnp.bfloat16)[:, :capacity]
        for e in range(local):
            row = tables[index, pl.ds(me * local + e, 1), :]
            scales[i, e] = jnp.transpose(jnp.broadcast_to(row, (tokens, tokens)))

    def pick(sources):
        places = []
        for i, (o, q) in enumerate(sources):
            index = q * chips + o
            place_tables(index, i)
            slot_row = tables[index, pl.ds(experts + me, 1), :]
            line = lax.broadcasted_iota(jnp.int32, (capacity, tokens), 0).astype(jnp.float32)
            places.append(jnp.where(slot_row == line, 1.0, 0.0).astype(jnp.bfloat16))

        def body(step, carry):
            at = pl.ds(pl.multiple_of(step * P_TILE, P_TILE), P_TILE)
            for i, (o, q) in enumerate(sources):
                picked[pl.ds(i * capacity, capacity), at] = jnp.dot(places[i], u_at(o, q)[:, at], preferred_element_type=jnp.float32).astype(jnp.bfloat16)
            return carry

        lax.fori_loop(0, width // P_TILE, body, 0)

    def down(base, group, offsets, keep, following, pass_on):
        sources = [(o, q) for q in range(CORES) for o in offsets]
        rows = len(sources) * capacity
        lines = pl.ds(keep, len(offsets))

        def pair_copy(block):
            slot = lax.rem(block, S_SLOTS)
            return remote(stage.at[slot, pl.ds(0, len(offsets))], landed.at[block, lines], pair_send.at[slot], pair_recv.at[group, block], 0, 1)

        def combine(block):
            for i, (o, q) in enumerate(sources):
                total = None
                for e in range(local):
                    scale = jnp.concatenate([scales[i, e]] * (D_TILE // tokens), axis=1)
                    piece = jnp.dot(spread[i], eout[e, pl.ds(i * capacity, capacity), :], preferred_element_type=jnp.float32) * scale
                    total = piece if total is None else total + piece
                if q == 0:
                    agg[o, block] = total
                else:
                    stage[lax.rem(block, S_SLOTS), offsets.index(o)] = total

        def body(step, carry):
            @pl.when((step > S_SLOTS) & (step <= steps_d))
            def _():
                pair_copy(step - 1 - S_SLOTS).wait_send()

            @pl.when(step < steps_d)
            def _():
                slot = stream(step, steps_d, base, expert_out, following)
                combine(jnp.maximum(step - 1, 0))
                for e in range(local):
                    for h in range(cols):
                        eout[e, pl.ds(0, rows), pl.ds(h * F_TILE, F_TILE)] = jnp.dot(act[e, pl.ds(0, rows), :], wbuf[slot, e, pl.ds(h * ff, ff), :], preferred_element_type=jnp.float32).astype(jnp.bfloat16)

            @pl.when(step == steps_d)
            def _():
                combine(step - 1)

            @pl.when((step >= 1) & (step <= steps_d))
            def _():
                pair_copy(step - 1).start()

            if pass_on is not None:
                @pl.when(step >= 4)
                def _():
                    pass_on(step - 4)

            @pl.when((step >= 3) & (step <= steps_d + 2))
            def _():
                block = step - 3
                pair_copy(block).wait_recv()
                for k, o in enumerate(offsets):
                    agg[o, block] = agg[o, block] + landed[block, keep + k]

            return carry

        lax.fori_loop(0, steps_d + (4 if pass_on is not None else 3), body, 0)
        for block in range(steps_d - S_SLOTS, steps_d):
            pair_copy(block).wait_send()

    def to_plus(src, dst, recv, send, block):
        return remote(src.at[block], dst.at[block], send.at[block], recv.at[block], plus, 0)

    def to_minus(src, dst, recv, send, block):
        return remote(src.at[block], dst.at[block], send.at[block], recv.at[block], minus, 0)

    def even_odd(block, even, odd):
        @pl.when(lax.rem(block, 2) == 0)
        def _():
            even()

        @pl.when(lax.rem(block, 2) == 1)
        def _():
            odd()

    def near_even(block):
        return to_minus(agg.at[minus], two_minus, minus_recv, near_send, block)

    def near_odd(block):
        return to_plus(agg.at[plus], two_plus, plus_recv, near_send, block)

    def far_even(block):
        return to_plus(agg.at[far], one_in, one_recv, one_send, block)

    def far_odd(block):
        return to_minus(agg.at[far], one_in, one_recv, one_send, block)

    def last_even(block):
        return to_plus(agg.at[plus], two_plus, plus_recv, two_send, block)

    def last_odd(block):
        return to_minus(agg.at[minus], two_minus, minus_recv, two_send, block)

    with jax.named_scope('rows_in'):
        forward('plus1', 'plus1_pair')
        forward('minus0', 'minus0_pair')
        for k in range(len(peers)):
            table_copy(k).wait_recv()
        tables[0] = table_ref[...]
        for name in ('plus0_pair', 'minus1_pair', 'plus1_pair', 'minus0_pair'):
            u_copy(name).wait_recv()

    def far_halves():
        forward('far0', 'far0_pair')
        forward('far1', 'far1_pair')

    near = (plus, minus)
    with jax.named_scope('pick1'):
        pick([(o, q) for q in range(CORES) for o in near])
    with jax.named_scope('gate_up1'):
        gate_up(near_base, picked, 2 * len(near) * capacity, act, expert_in, expert_out, lambda step: at_step(step, steps_f * 3 // 4, far_halves))
    with jax.named_scope('down1'):
        down(near_base + steps_f, 0, near, 0, expert_in,
             lambda block: even_odd(block, lambda: near_even(block).start(), lambda: near_odd(block).start()))
        pl.semaphore_signal(credit, inc=1, device_id={'ep': peer(0, 1)}, device_id_type=MESH)

    with jax.named_scope('pick2'):
        for name in ('far0_pair', 'far1_pair', 'own'):
            u_copy(name).wait_recv()
        pick([(far, 0), (far, 1)])
    with jax.named_scope('gate_up2'):
        gate_up(far_base, picked, 2 * capacity, act, expert_in, expert_out, None)
        pl.semaphore_wait(credit, 1)
    with jax.named_scope('down2'):
        down(far_base + steps_f, 1, (far,), 0, expert_in,
             lambda block: even_odd(block, lambda: far_even(block).start(), lambda: far_odd(block).start()))

    def relay(block):
        def even():
            far_even(block).wait_recv()
            agg[plus, block] = agg[plus, block] + one_in[block]
            last_even(block).start()

        def odd():
            far_odd(block).wait_recv()
            agg[minus, block] = agg[minus, block] + one_in[block]
            last_odd(block).start()

        even_odd(block, even, odd)

    def relay_late(step):
        @pl.when(step >= steps_f - steps_d)
        def _():
            relay(step - (steps_f - steps_d))

    with jax.named_scope('pick3'):
        pick([(0, 0), (0, 1)])
    with jax.named_scope('gate_up3'):
        gate_up(own_base, picked, 2 * capacity, act, expert_in, expert_out, relay_late)
    with jax.named_scope('down3'):
        down(own_base + steps_f, 2, (0,), 1, lambda step, slot: shared_down(step + early, slot), None)
    with jax.named_scope('shared_rest'):
        shared_out(rest_base, early, steps_d, None)

    def final_body(block, carry):
        last_even(block).wait_recv()
        last_odd(block).wait_recv()
        at = pl.ds(pl.multiple_of(block * D_TILE, D_TILE), D_TILE)
        routed = agg[0, block] + two_plus[block] + two_minus[block]
        out_ref[:, at] = (mid_ref[:, at].astype(jnp.float32) + routed + out_ref[:, at].astype(jnp.float32)).astype(jnp.bfloat16)

        def even():
            near_even(block).wait_send()
            far_even(block).wait_send()
            last_even(block).wait_send()

        def odd():
            near_odd(block).wait_send()
            far_odd(block).wait_send()
            last_odd(block).wait_send()

        even_odd(block, even, odd)
        return carry

    with jax.named_scope('final'):
        lax.fori_loop(0, steps_d, final_body, 0)
        for k in range(len(peers)):
            table_copy(k).wait_send()
        for name in routes:
            u_copy(name).wait_send()


def moe_block(u_norm, x_mid, table, w_gate, w_up, w_down, shared_gate, shared_up, shared_down, ep_size, capacity):
    tokens, width = u_norm.shape
    local, _, ff = w_gate.shape
    chips = ep_size // CORES
    blocks = width // D_TILE
    rows = CORES * 2 * capacity
    f32, bf16 = jnp.float32, jnp.bfloat16
    dma = pltpu.SemaphoreType.DMA
    vmem = pl.BlockSpec(memory_space=pltpu.VMEM)
    hbm = pl.BlockSpec(memory_space=pl.ANY)
    return pl.pallas_call(
        functools.partial(moe_kernel, chips, capacity),
        out_shape=jax.ShapeDtypeStruct((tokens, width), bf16),
        in_specs=[vmem] * 3 + [hbm] * 6,
        out_specs=vmem,
        scratch_shapes=[
            pltpu.VMEM((ep_size - 1, tokens, width), bf16),
            pltpu.VMEM((rows, width), bf16),
            pltpu.VMEM((local, rows, ff), bf16),
            pltpu.VMEM((local, tokens, ff), bf16),
            pltpu.VMEM((W_SLOTS, local, width, F_TILE), bf16),
            pltpu.VMEM((local, rows, D_TILE), bf16),
            pltpu.VMEM((chips, blocks, tokens, D_TILE), f32),
            pltpu.VMEM((S_SLOTS, 2, tokens, D_TILE), f32),
            pltpu.VMEM((blocks, 2, tokens, D_TILE), f32),
            pltpu.VMEM((blocks, tokens, D_TILE), f32),
            pltpu.VMEM((blocks, tokens, D_TILE), f32),
            pltpu.VMEM((blocks, tokens, D_TILE), f32),
            pltpu.VMEM((ep_size,) + table.shape, f32),
            pltpu.VMEM((2 * CORES, local, tokens, tokens), f32),
            pltpu.VMEM((2 * CORES, tokens, capacity), bf16),
            dma((W_SLOTS, 2 * local)),
            dma((ep_size - 1,)), dma((ep_size,)),
            dma((13,)), dma((13,)),
            dma((S_SLOTS,)), dma((3, blocks)),
            dma((blocks,)), dma((blocks,)), dma((blocks,)), dma((blocks,)), dma((blocks,)), dma((blocks,)),
            pltpu.SemaphoreType.REGULAR,
        ],
        compiler_params=pltpu.CompilerParams(collective_id=0, has_side_effects=True, vmem_limit_bytes=67043328),
        name='moe',
    )(u_norm, x_mid, table, w_gate, w_up, w_down, shared_gate, shared_up, shared_down)


def solution(mesh):
    ep_size = mesh.shape['ep']
    batch = P(('dp', 'ep'))
    whole = P()
    by_expert = P('ep')

    def local_step(hidden, positions, ckv_cache, kpe_cache, topk_ids, attn_gain, w_dq, q_gain, w_uq, w_dkv, kv_gain, w_uk, w_uv, w_out, ffn_gain, w_router, w_gate, w_up, w_down, shared_gate, shared_up, shared_down):
        x_mid, c_new, k_new = attention_block(hidden, positions, ckv_cache, kpe_cache, attn_gain, w_dq, q_gain, w_uq, w_dkv, kv_gain, w_uk, w_uv, w_out)
        u_norm = rms_norm(x_mid, ffn_gain).astype(jnp.bfloat16)
        experts = w_router.shape[1]
        capacity = (CAP_FACTOR * topk_ids.size + experts - 1) // experts
        table = route_table(u_norm, topk_ids, w_router, w_gate.shape[0], capacity)
        hidden_out = moe_block(u_norm, x_mid, table, w_gate, w_up, w_down, shared_gate, shared_up, shared_down, ep_size, capacity)
        return hidden_out, c_new, k_new

    in_specs = (batch,) * 5 + (whole,) * 11 + (by_expert,) * 3 + (whole,) * 3
    return jax.shard_map(local_step, mesh=mesh, in_specs=in_specs, out_specs=(batch, batch, batch), check_vma=False)
```

time: 301 us -> 262 us (0.87)
  matrix products: 68.5 us -> 29.3 us
  local copies, waits for them, and re-layouts: 15.7 us -> 12.6 us
    dot_general x7 -> x2, matrix products: 42.2 us -> 3.15 us  [the longest x1 2.4 us: attention_block(): jnp.einsum('htc,chv->thv', context, w_uv.reshape(kv_rank, heads, VALUE_DI...]
    pallas_call x0 -> x1, Pallas kernels: none -> 35.1 us  [attend(): pl.pallas_call(functools.partial(attend_kernel, heads), grid=(tokens // s...]
    pallas_call x1, Pallas kernels: 207 us -> 175 us  [moe_block(): pl.pallas_call(functools.partial(moe_kernel, chips, capacity), out_shape=...]
    unnamed x51 -> x23, local copies, waits for them, and re-layouts: 7.15 us -> 7.52 us
where the time goes in v2:
time: 262 us
  Pallas kernels  210 us (80%)
  matrix products  29.3 us (11%)
  local copies, waits for them, and re-layouts  12.6 us (5%)
  other arithmetic  8.7 us (3%)
    pallas_call x1, Pallas kernels, moe_block(): pl.pallas_call(functools.partial(moe_kernel, chips, capacity), out_shape=...  175 us
    pallas_call x1, Pallas kernels, attend(): pl.pallas_call(functools.partial(attend_kernel, heads), grid=(tokens // s...  35.1 us
    dot_general x1, matrix products, attention_block(): jnp.dot(heads_out.reshape(tokens, heads * VALUE_DIM), w_out, preferred_el...  10.4 us
    dot_general x1, matrix products, attention_block(): jnp.dot(normed, w_dq, preferred_element_type=jnp.float32)  8.34 us
    unnamed x23, local copies, waits for them, and re-layouts  7.52 us

profile of v2, /device:TPU:112, one launch (start us, length us, event | category | flops | bytes accessed | tf_op | source)
XLA Modules:
  0.0 261.9 jit_solution(16199277173652944671)
XLA Ops:
  0.6 0.7 convert_element_type.78
  1.3 1.6 fusion.4
  3.0 0.7 fusion.24
  3.7 0.7 convert_element_type.80
  4.4 0.1 and_select_fusion
  4.5 0.7 convert_element_type.73
  5.2 0.7 convert_element_type.71
  5.9 0.7 convert_element_type.86
  6.6 0.8 copy.59.position_ref
  7.4 5.2 %fusion.19 = f32[128,576]{1,0:T(8,128)S(1)} fusion(bf16[5120,576]{0,1:T(8,128)(2,1)} %param.31, bf16[128,5120]{1,0:T(8,128)(2,1)} %param.22, f32[5120]{0:T(1024)S(1)} %convert_element_type.71, f32[128]{0:T(128)S(1)} %add_rsqrt_fusion.3), kind=kOutput, calls=%fused_computation.31 | convolution fusion | flops 757596160 | bytes 7524864 | tf_op jit(solution)/shard_map/dot_general | solution.py:126
  12.6 0.1 multiply_reduce_fusion.1
  12.8 0.1 multiply_convert_fusion.2.c_new_ref
  12.9 0.0 copy-start.1
  12.9 0.0 slice-start
  12.9 0.3 subtract_convert_fusion.1
  13.2 0.1 pad_maximum_fusion.2
  13.3 0.1 pad_maximum_fusion.1.k_new_ref
  13.4 0.7 copy.61
  14.1 8.3 %multiply_reduce_fusion = (f32[128]{0:T(128)S(1)}, f32[128,1536]{1,0:T(8,128)S(1)}) fusion(bf16[5120,1536]{1,0:T(8,128)(2,1)} %param.28, bf16[128,5120]{1,0:T(8,128)(2,1)} %param.22, f32[5120]{0:T(1024)S(1)} %convert_element_type.71, f32[128]{0:T(128)S(1)} %add_rsqrt_fusion.3), kind=kOutput, calls=%fused_computation.25 | convolution fusion | flops 2016280448 | bytes 17847296 | tf_op jit(solution)/shard_map/dot_general | solution.py:122
  22.5 0.0 slice-done
  22.5 0.0 slice-done.1
  22.5 0.0 slice-done.2
  22.5 1.5 convolution_convert_fusion
  24.0 0.4 copy.51
  24.4 0.3 copy.65
  24.7 0.1 convert_element_type.77
  24.8 0.0 copy-start.5
  24.8 0.5 subtract_convert_fusion
  25.3 0.3 maximum_bitcast_fusion
  25.6 0.3 pad_maximum_fusion.q_rot_ref
  25.9 0.5 copy-done.5
  26.4 0.8 fusion.10.q_abs_ref
  27.1 0.0 copy-done.1
  27.2 1.4 copy-done
  28.6 35.1 %attend.1 = bf16[16,128,512]{2,1,0:T(8,128)(2,1)S(1)} custom-call(s32[128,1]{1,0:T(8,128)S(1)} %copy.59.position_ref, bf16[16,128,512]{2,1,0:T(8,128)(2,1)S(1)} %fusion.10.q_abs_ref, bf16[16,128,128]{2,1,0:T(8,128)(2,1)S(1)} %pad_maximum_fusion.q_rot_ref, bf16[128,256,512]{2,1,0:T(8,128)(2,1)} %ckv_ref.1, bf16[128,64,256]{2,1,0:T(8,128)(2,1)S(1)} %bitcast.30, ...), custom_call_target="tpu_custom_call" | custom-call | tf_op jit(solution)/shard_map/attend/pallas_call | solution.py:97
  63.7 3.9 %copy.63 = bf16[512,2048]{0,1:T(8,128)(2,1)} copy(bf16[512,2048]{1,0:T(8,128)(2,1)} %param.34) | data formatting | bytes 4194304 | tf_op jit(solution)/shard_map/reshape | solution.py:131
  67.7 2.4 convolution_convert_fusion.1
  70.1 10.4 %fusion.1 = (f32[128]{0:T(128)S(1)}, bf16[128,5120]{1,0:T(8,128)(2,1)S(1)}) fusion(bf16[128,2048]{0,1:T(8,128)(2,1)S(1)} %bitcast.36, bf16[2048,5120]{1,0:T(8,128)(2,1)} %param.35, bf16[128,5120]{1,0:T(8,128)(2,1)S(1)} %copy-done.2), kind=kOutput, calls=%fused_computation.7 | convolution fusion | flops 2688286720 | bytes 24117760 | tf_op jit(solution)/shard_map/dot_general | solution.py:132
  80.5 0.0 copy-start.3
  80.5 0.0 copy-start.6
  80.6 1.0 copy-done.3
  81.6 0.4 fusion.3.u_ref
  82.0 0.0 copy-start.4
  82.0 1.0 copy-done.4
  83.1 0.5 select_reduce_fusion
  83.6 0.6 maximum_bitcast_fusion.1.table_ref
  84.2 175.2 %moe.1 = bf16[128,5120]{1,0:T(8,128)(2,1)} custom-call(bf16[128,5120]{1,0:T(8,128)(2,1)} %copy-done.4, bf16[128,5120]{1,0:T(8,128)(2,1)} %copy-done.3, f32[24,128]{1,0:T(8,128)} %maximum_bitcast_fusion.1.table_ref, bf16[2,5120,1536]{2,1,0:T(8,128)(2,1)} %gate_ref.1, bf16[2,5120,1536]{2,1,0:T(8,128)(2,1)} %up_ref.1, bf16[2,1536,5120]{2,1,0:T(8,128)(2,1)} %down_ref.1, ...), custom_call_target="tpu_custom_call" | custom-call | tf_op jit(solution)/shard_map/moe/pallas_call | solution.py:540
  259.4 2.5 copy.74
  (15 shorter events, 0.1 us)
Async XLA Ops:
  12.9 14.3 %copy-start.1 = (bf16[128,512]{1,0:T(8,128)(2,1)}, bf16[128,512]{1,0:T(8,128)(2,1)S(1)}, u32[]{:S(2)}) copy-start(bf16[128,512]{1,0:T(8,128)(2,1)S(1)} %multiply_convert_fusion.2.c_new_ref) | copy-start | bytes 393220
  12.9 9.6 %slice-start = ((s8[9437184]{0:T(1024)(128)(4,1)}), s8[1048576]{0:T(1024)(128)(4,1)S(1)}, s32[]{:S(2)}) async-start(s8[9437184]{0:T(1024)(128)(4,1)} %bitcast.31), calls=%async_computation | async-start | bytes 2097152
  14.1 8.4 %slice-start.1 = ((s8[9437184]{0:T(1024)(128)(4,1)}), s8[4194304]{0:T(1024)(128)(4,1)S(1)}, s32[]{:S(2)}) async-start(s8[9437184]{0:T(1024)(128)(4,1)} %bitcast.31), calls=%async_computation.1 | async-start | bytes 8388608
  14.1 8.4 %slice-start.2 = ((s8[9437184]{0:T(1024)(128)(4,1)}), s8[4194304]{0:T(1024)(128)(4,1)S(1)}, s32[]{:S(2)}) async-start(s8[9437184]{0:T(1024)(128)(4,1)} %bitcast.31), calls=%async_computation.2 | async-start | bytes 8388608
  24.8 1.6 copy-start.5
  26.4 2.2 copy-start
  67.7 2.4 copy-start.2
  80.5 1.1 copy-start.3
  80.5 2.5 copy-start.6
  82.0 1.1 copy-start.4

commit v3 on v2

--- a/solution.py
+++ b/solution.py
@@ -22,6 +22,7 @@
 S_SLOTS = 3
 P_TILE = 1024
 SEQS = 8
+HEADS_STEP = 2
 PARTS = 2
 MESH = pl.DeviceIdType.MESH
 
@@ -54,13 +55,16 @@
     def per_row(block):
         return jnp.concatenate([block] * heads, axis=0)
 
+    q_all = jnp.concatenate([q_abs_ref[:, pl.ds(part * SEQS, SEQS), :].reshape(rows, kv_rank) for part in range(PARTS)], axis=0)
+    everything = lax.dot_general(ckv_ref[...].reshape(PARTS * SEQS * cache_len, kv_rank), q_all, (((1,), (1,)), ((), ())), preferred_element_type=f32)
+    for part in range(PARTS):
+        raw[part] = everything[part * SEQS * cache_len:(part + 1) * SEQS * cache_len, part * rows:(part + 1) * rows]
     row_seq = lax.broadcasted_iota(jnp.int32, (rows, 1), 0) % SEQS
     for part in range(PARTS):
         seqs = pl.ds(part * SEQS, SEQS)
         q_abs = q_abs_ref[:, seqs, :].reshape(rows, kv_rank)
         q_rot = q_rot_ref[:, seqs, :].reshape(rows, wide)
         ckv = ckv_ref[seqs].reshape(SEQS * cache_len, kv_rank)
-        raw[part] = lax.dot_general(ckv, q_abs, (((1,), (1,)), ((), ())), preferred_element_type=f32)
         lane_seq = lax.broadcasted_iota(jnp.int32, (cache_len, rows), 1) % SEQS
         scores = raw[part, pl.ds(0, cache_len)]
         for g in range(1, SEQS):
@@ -114,7 +118,54 @@
     )(positions[:, None], q_abs, doubled, ckv_cache, jnp.swapaxes(kpe_cache, 1, 2), c_new, k_doubled)
 
 
-def attention_block(hidden, positions, ckv_cache, kpe_cache, attn_gain, w_dq, q_gain, w_uq, w_dkv, kv_gain, w_uk, w_uv, w_out):
+def norm_rows(vec, gain):
+    return vec * lax.rsqrt(jnp.mean(vec * vec, axis=1, keepdims=True) + EPSILON) * gain.astype(jnp.float32)
+
+
+def out_proj_kernel(context_ref, uv_ref, out_ref, hidden_ref, gain_ref, mid_ref, u_ref, total):
+    step = pl.program_id(0)
+    width = hidden_ref.shape[1]
+
+    @pl.when(step == 0)
+    def _():
+        total[...] = hidden_ref[...].astype(jnp.float32)
+
+    heads = [jnp.dot(context_ref[k], uv_ref[:, k * VALUE_DIM:(k + 1) * VALUE_DIM], preferred_element_type=jnp.float32) for k in range(context_ref.shape[0])]
+    heads = jnp.concatenate(heads, axis=1).astype(jnp.bfloat16)
+    for c in range(0, width, P_TILE):
+        total[:, c:c + P_TILE] += jnp.dot(heads, out_ref[:, c:c + P_TILE], preferred_element_type=jnp.float32)
+
+    @pl.when(step == pl.num_programs(0) - 1)
+    def _():
+        mid = total[...].astype(jnp.bfloat16)
+        mid_ref[...] = mid
+        u_ref[...] = norm_rows(mid.astype(jnp.float32), gain_ref[...]).astype(jnp.bfloat16)
+
+
+def out_proj(context, w_uv, w_out, hidden, ffn_gain):
+    heads, tokens, kv_rank = context.shape
+    width = hidden.shape[1]
+    whole = lambda shape: pl.BlockSpec(shape, lambda i: (0, 0))
+    rows = jax.ShapeDtypeStruct((tokens, width), jnp.bfloat16)
+    return pl.pallas_call(
+        out_proj_kernel,
+        grid=(heads // HEADS_STEP,),
+        out_shape=(rows, rows),
+        in_specs=[
+            pl.BlockSpec((HEADS_STEP, tokens, kv_rank), lambda i: (i, 0, 0)),
+            pl.BlockSpec((kv_rank, HEADS_STEP * VALUE_DIM), lambda i: (0, i)),
+            pl.BlockSpec((HEADS_STEP * VALUE_DIM, width), lambda i: (i, 0)),
+            whole((tokens, width)),
+            whole((1, width)),
+        ],
+        out_specs=(whole((tokens, width)), whole((tokens, width))),
+        scratch_shapes=[pltpu.VMEM((tokens, width), jnp.float32)],
+        compiler_params=pltpu.CompilerParams(dimension_semantics=('arbitrary',), vmem_limit_bytes=32 * 2**20),
+        name='out_proj',
+    )(context, w_uv, w_out, hidden, ffn_gain[None])
+
+
+def attention_block(hidden, positions, ckv_cache, kpe_cache, attn_gain, w_dq, q_gain, w_uq, w_dkv, kv_gain, w_uk, w_uv, w_out, ffn_gain):
     tokens = hidden.shape[0]
     kv_rank = w_uk.shape[0]
     heads = w_uk.shape[1] // NOPE_DIM
@@ -128,10 +179,8 @@
     k_new = rotary(kv_proj[:, kv_rank:], positions).astype(jnp.bfloat16)
     q_abs = jnp.einsum('thn,chn->htc', q_nope, w_uk.reshape(kv_rank, heads, NOPE_DIM), preferred_element_type=jnp.float32).astype(jnp.bfloat16)
     context = attend(q_abs, jnp.swapaxes(q_rot, 0, 1), ckv_cache, kpe_cache, c_new, k_new, positions)
-    heads_out = jnp.einsum('htc,chv->thv', context, w_uv.reshape(kv_rank, heads, VALUE_DIM), preferred_element_type=jnp.float32).astype(jnp.bfloat16)
-    attn_out = jnp.dot(heads_out.reshape(tokens, heads * VALUE_DIM), w_out, preferred_element_type=jnp.float32)
-    x_mid = (hidden.astype(jnp.float32) + attn_out).astype(jnp.bfloat16)
-    return x_mid, c_new, k_new
+    x_mid, u_norm = out_proj(context, w_uv, w_out, hidden, ffn_gain)
+    return x_mid, u_norm, c_new, k_new
 
 
 def route_table(u_norm, topk_ids, w_router, local, capacity):
@@ -151,7 +200,7 @@
 
 def moe_kernel(chips, capacity, u_ref, mid_ref, table_ref, gate_ref, up_ref, down_ref, sgate_ref, sup_ref, sdown_ref, out_ref,
                far_u, picked, act, sact, wbuf, eout, agg, stage, landed, one_in, two_plus, two_minus, tables, scales, spread,
-               w_sem, table_send, table_recv, u_send, u_recv, pair_send, pair_recv, near_send, one_send, one_recv, two_send, plus_recv, minus_recv, credit):
+               w_sem, table_send, table_recv, u_send, u_recv, pair_send, pair_recv, near_send, one_send, one_recv, two_send, plus_recv, minus_recv, mid_sem, credit):
     tokens, width = u_ref.shape
     local, _, ff = gate_ref.shape
     experts = local * chips * CORES
@@ -231,22 +280,25 @@
         finish(load(step, slot))
         return slot
 
-    def gate_up(base, lhs, rows, into, load, following, hook):
+    def gate_up(base, lhs, rows, into, places, load, following, hook):
         def body(step, carry):
             slot = stream(step, steps_f, base, load, following)
             e, b = lax.div(step, f_blocks), lax.rem(step, f_blocks)
             h_gate = jnp.dot(lhs[:rows], wbuf[slot, 0], preferred_element_type=jnp.float32)
             h_up = jnp.dot(lhs[:rows], wbuf[slot, 1], preferred_element_type=jnp.float32)
-            into[e, pl.ds(0, rows), pl.ds(pl.multiple_of(b * F_TILE, F_TILE), F_TILE)] = (h_gate * jax.nn.sigmoid(h_gate) * h_up).astype(jnp.bfloat16)
+            value = (h_gate * jax.nn.sigmoid(h_gate) * h_up).astype(jnp.bfloat16)
+            size = rows // len(places)
+            for n, place in enumerate(places):
+                into[e, pl.ds(place, size), pl.ds(pl.multiple_of(b * F_TILE, F_TILE), F_TILE)] = value[n * size:(n + 1) * size]
             if hook is not None:
                 hook(step)
             return carry
 
         lax.fori_loop(0, steps_f, body, 0)
 
-    def shared_out(base, low, high, following):
+    def shared_out(base, following):
         def body(step, carry):
-            slot = stream(step, high, base - low, shared_down, following)
+            slot = stream(step, steps_d, base, shared_down, following)
             for h in range(cols):
                 total = None
                 for e in range(local):
@@ -255,7 +307,7 @@
                 out_ref[:, pl.ds(pl.multiple_of(step * D_TILE + h * F_TILE, F_TILE), F_TILE)] = total.astype(jnp.bfloat16)
             return carry
 
-        lax.fori_loop(low, high, body, 0)
+        lax.fori_loop(0, steps_d, body, 0)
 
     with jax.named_scope('enter'):
         start(ahead, shared_in, 0)
@@ -310,14 +362,12 @@
         forward('minus1', 'far1', 'minus1_pair')
 
     with jax.named_scope('shared_in'):
-        gate_up(0, u_ref, tokens, sact, shared_in, shared_down, lambda step: at_step(step, steps_f * 3 // 4, first_halves))
-    early = steps_d // 2
-    near_base = steps_f + early
+        gate_up(0, u_ref, tokens, sact, (0,), shared_in, shared_down, lambda step: at_step(step, steps_f * 3 // 4, first_halves))
+    near_base = steps_f + steps_d
     far_base = near_base + steps_f + steps_d
     own_base = far_base + steps_f + steps_d
-    rest_base = own_base + steps_f + steps_d
     with jax.named_scope('shared_out'):
-        shared_out(steps_f, 0, early, expert_in)
+        shared_out(steps_f, expert_in)
 
     def place_tables(index, i):
         slot_row = tables[index, pl.ds(experts + me, 1), :]
@@ -328,9 +378,9 @@
             row = tables[index, pl.ds(me * local + e, 1), :]
             scales[i, e] = jnp.transpose(jnp.broadcast_to(row, (tokens, tokens)))
 
-    def pick(sources):
+    def pick(sources, kept):
         places = []
-        for i, (o, q) in enumerate(sources):
+        for i, (o, q) in zip(kept, sources):
             index = q * chips + o
             place_tables(index, i)
             slot_row = tables[index, pl.ds(experts + me, 1), :]
@@ -345,28 +395,35 @@
 
         lax.fori_loop(0, width // P_TILE, body, 0)
 
-    def down(base, group, offsets, keep, following, pass_on):
-        sources = [(o, q) for q in range(CORES) for o in offsets]
-        rows = len(sources) * capacity
-        lines = pl.ds(keep, len(offsets))
+    def down(base, group, chips_in, keep, first, offset, following, pass_on, lag):
+        rows = chips_in * CORES * capacity
+        lines = pl.ds(keep, chips_in)
 
         def pair_copy(block):
             slot = lax.rem(block, S_SLOTS)
-            return remote(stage.at[slot, pl.ds(0, len(offsets))], landed.at[block, lines], pair_send.at[slot], pair_recv.at[group, block], 0, 1)
+            return remote(stage.at[slot, pl.ds(0, chips_in)], landed.at[block, lines], pair_send.at[slot], pair_recv.at[group, block], 0, 1)
 
         def combine(block):
-            for i, (o, q) in enumerate(sources):
-                total = None
-                for e in range(local):
-                    scale = jnp.concatenate([scales[i, e]] * (D_TILE // tokens), axis=1)
-                    piece = jnp.dot(spread[i], eout[e, pl.ds(i * capacity, capacity), :], preferred_element_type=jnp.float32) * scale
-                    total = piece if total is None else total + piece
-                if q == 0:
-                    agg[o, block] = total
-                else:
-                    stage[lax.rem(block, S_SLOTS), offsets.index(o)] = total
+            for k in range(chips_in):
+                for q in range(CORES):
+                    i = k * CORES + q
+                    source = first(block) + i
+                    total = None
+                    for e in range(local):
+                        scale = jnp.concatenate([scales[source, e]] * (D_TILE // tokens), axis=1)
+                        piece = jnp.dot(spread[source], eout[e, pl.ds(i * capacity, capacity), :], preferred_element_type=jnp.float32) * scale
+                        total = piece if total is None else total + piece
+                    if q == 0:
+                        agg[offset(block, k), block] = total
+                    else:
+                        stage[lax.rem(block, S_SLOTS), k] = total
 
         def body(step, carry):
+            if pass_on is not None:
+                @pl.when(step > lag)
+                def _():
+                    pass_on(step - 1 - lag)
+
             @pl.when((step > S_SLOTS) & (step <= steps_d))
             def _():
                 pair_copy(step - 1 - S_SLOTS).wait_send()
@@ -375,9 +432,10 @@
             def _():
                 slot = stream(step, steps_d, base, expert_out, following)
                 combine(jnp.maximum(step - 1, 0))
+                lines_in = pl.ds(pl.multiple_of(first(step) * capacity, CORES * capacity), rows)
                 for e in range(local):
                     for h in range(cols):
-                        eout[e, pl.ds(0, rows), pl.ds(h * F_TILE, F_TILE)] = jnp.dot(act[e, pl.ds(0, rows), :], wbuf[slot, e, pl.ds(h * ff, ff), :], preferred_element_type=jnp.float32).astype(jnp.bfloat16)
+                        eout[e, pl.ds(0, rows), pl.ds(h * F_TILE, F_TILE)] = jnp.dot(act[e, lines_in, :], wbuf[slot, e, pl.ds(h * ff, ff), :], preferred_element_type=jnp.float32).astype(jnp.bfloat16)
 
             @pl.when(step == steps_d)
             def _():
@@ -387,21 +445,17 @@
             def _():
                 pair_copy(step - 1).start()
 
-            if pass_on is not None:
-                @pl.when(step >= 4)
-                def _():
-                    pass_on(step - 4)
-
-            @pl.when((step >= 3) & (step <= steps_d + 2))
+            @pl.when((step >= lag) & (step < steps_d + lag))
             def _():
-                block = step - 3
+                block = step - lag
                 pair_copy(block).wait_recv()
-                for k, o in enumerate(offsets):
+                for k in range(chips_in):
+                    o = offset(block, k)
                     agg[o, block] = agg[o, block] + landed[block, keep + k]
 
             return carry
 
-        lax.fori_loop(0, steps_d + (4 if pass_on is not None else 3), body, 0)
+        lax.fori_loop(0, steps_d + lag + (1 if pass_on is not None else 0), body, 0)
         for block in range(steps_d - S_SLOTS, steps_d):
             pair_copy(block).wait_send()
 
@@ -451,26 +505,25 @@
         forward('far0', 'far0_pair')
         forward('far1', 'far1_pair')
 
-    near = (plus, minus)
     with jax.named_scope('pick1'):
-        pick([(o, q) for q in range(CORES) for o in near])
+        pick([(plus, 0), (plus, 1), (minus, 0), (minus, 1)], (0, 1, 4, 5))
     with jax.named_scope('gate_up1'):
-        gate_up(near_base, picked, 2 * len(near) * capacity, act, expert_in, expert_out, lambda step: at_step(step, steps_f * 3 // 4, far_halves))
+        gate_up(near_base, picked, 4 * capacity, act, (0, 4 * capacity), expert_in, expert_out, lambda step: at_step(step, steps_f * 3 // 4, far_halves))
     with jax.named_scope('down1'):
-        down(near_base + steps_f, 0, near, 0, expert_in,
-             lambda block: even_odd(block, lambda: near_even(block).start(), lambda: near_odd(block).start()))
+        down(near_base + steps_f, 0, 1, 1, lambda block: (1 - lax.rem(block, 2)) * 2 * CORES, lambda block, k: plus + (1 - lax.rem(block, 2)) * (minus - plus), expert_in,
+             lambda block: even_odd(block, lambda: near_even(block).start(), lambda: near_odd(block).start()), 3)
         pl.semaphore_signal(credit, inc=1, device_id={'ep': peer(0, 1)}, device_id_type=MESH)
 
     with jax.named_scope('pick2'):
         for name in ('far0_pair', 'far1_pair', 'own'):
             u_copy(name).wait_recv()
-        pick([(far, 0), (far, 1)])
+        pick([(far, 0), (far, 1)], (2, 3))
     with jax.named_scope('gate_up2'):
-        gate_up(far_base, picked, 2 * capacity, act, expert_in, expert_out, None)
+        gate_up(far_base, picked, 2 * capacity, act, (2 * capacity,), expert_in, expert_out, None)
         pl.semaphore_wait(credit, 1)
     with jax.named_scope('down2'):
-        down(far_base + steps_f, 1, (far,), 0, expert_in,
-             lambda block: even_odd(block, lambda: far_even(block).start(), lambda: far_odd(block).start()))
+        down(far_base + steps_f, 1, 2, 0, lambda block: lax.rem(block, 2) * CORES, lambda block, k: plus + lax.rem(block, 2) + k, expert_in,
+             lambda block: even_odd(block, lambda: far_even(block).start(), lambda: far_odd(block).start()), 2)
 
     def relay(block):
         def even():
@@ -490,21 +543,24 @@
         def _():
             relay(step - (steps_f - steps_d))
 
+    pl.semaphore_signal(credit, inc=1, device_id={'ep': peer(0, 1)}, device_id_type=MESH)
     with jax.named_scope('pick3'):
-        pick([(0, 0), (0, 1)])
+        pick([(0, 0), (0, 1)], (0, 1))
     with jax.named_scope('gate_up3'):
-        gate_up(own_base, picked, 2 * capacity, act, expert_in, expert_out, relay_late)
+        gate_up(own_base, picked, 2 * capacity, act, (0,), expert_in, expert_out, relay_late)
+    late_mid = u_at(far, 1)
+    mid_copy = pltpu.make_async_copy(mid_ref, late_mid, mid_sem)
+    mid_copy.start()
     with jax.named_scope('down3'):
-        down(own_base + steps_f, 2, (0,), 1, lambda step, slot: shared_down(step + early, slot), None)
-    with jax.named_scope('shared_rest'):
-        shared_out(rest_base, early, steps_d, None)
+        pl.semaphore_wait(credit, 1)
+        down(own_base + steps_f, 2, 1, 0, lambda block: 0, lambda block, k: 0, None, None, 3)
 
     def final_body(block, carry):
         last_even(block).wait_recv()
         last_odd(block).wait_recv()
         at = pl.ds(pl.multiple_of(block * D_TILE, D_TILE), D_TILE)
         routed = agg[0, block] + two_plus[block] + two_minus[block]
-        out_ref[:, at] = (mid_ref[:, at].astype(jnp.float32) + routed + out_ref[:, at].astype(jnp.float32)).astype(jnp.bfloat16)
+        out_ref[:, at] = (late_mid[:, at].astype(jnp.float32) + routed + out_ref[:, at].astype(jnp.float32)).astype(jnp.bfloat16)
 
         def even():
             near_even(block).wait_send()
@@ -520,6 +576,7 @@
         return carry
 
     with jax.named_scope('final'):
+        mid_copy.wait()
         lax.fori_loop(0, steps_d, final_body, 0)
         for k in range(len(peers)):
             table_copy(k).wait_send()
@@ -540,12 +597,12 @@
     return pl.pallas_call(
         functools.partial(moe_kernel, chips, capacity),
         out_shape=jax.ShapeDtypeStruct((tokens, width), bf16),
-        in_specs=[vmem] * 3 + [hbm] * 6,
+        in_specs=[vmem, hbm, vmem] + [hbm] * 6,
         out_specs=vmem,
         scratch_shapes=[
             pltpu.VMEM((ep_size - 1, tokens, width), bf16),
             pltpu.VMEM((rows, width), bf16),
-            pltpu.VMEM((local, rows, ff), bf16),
+            pltpu.VMEM((local, 3 * CORES * capacity, ff), bf16),
             pltpu.VMEM((local, tokens, ff), bf16),
             pltpu.VMEM((W_SLOTS, local, width, F_TILE), bf16),
             pltpu.VMEM((local, rows, D_TILE), bf16),
@@ -556,14 +613,14 @@
             pltpu.VMEM((blocks, tokens, D_TILE), f32),
             pltpu.VMEM((blocks, tokens, D_TILE), f32),
             pltpu.VMEM((ep_size,) + table.shape, f32),
-            pltpu.VMEM((2 * CORES, local, tokens, tokens), f32),
-            pltpu.VMEM((2 * CORES, tokens, capacity), bf16),
+            pltpu.VMEM((3 * CORES, local, tokens, tokens), f32),
+            pltpu.VMEM((3 * CORES, tokens, capacity), bf16),
             dma((W_SLOTS, 2 * local)),
             dma((ep_size - 1,)), dma((ep_size,)),
             dma((13,)), dma((13,)),
             dma((S_SLOTS,)), dma((3, blocks)),
             dma((blocks,)), dma((blocks,)), dma((blocks,)), dma((blocks,)), dma((blocks,)), dma((blocks,)),
-            pltpu.SemaphoreType.REGULAR,
+            dma(()), pltpu.SemaphoreType.REGULAR,
         ],
         compiler_params=pltpu.CompilerParams(collective_id=0, has_side_effects=True, vmem_limit_bytes=67043328),
         name='moe',
@@ -577,8 +634,7 @@
     by_expert = P('ep')
 
     def local_step(hidden, positions, ckv_cache, kpe_cache, topk_ids, attn_gain, w_dq, q_gain, w_uq, w_dkv, kv_gain, w_uk, w_uv, w_out, ffn_gain, w_router, w_gate, w_up, w_down, shared_gate, shared_up, shared_down):
-        x_mid, c_new, k_new = attention_block(hidden, positions, ckv_cache, kpe_cache, attn_gain, w_dq, q_gain, w_uq, w_dkv, kv_gain, w_uk, w_uv, w_out)
-        u_norm = rms_norm(x_mid, ffn_gain).astype(jnp.bfloat16)
+        x_mid, u_norm, c_new, k_new = attention_block(hidden, positions, ckv_cache, kpe_cache, attn_gain, w_dq, q_gain, w_uq, w_dkv, kv_gain, w_uk, w_uv, w_out, ffn_gain)
         experts = w_router.shape[1]
         capacity = (CAP_FACTOR * topk_ids.size + experts - 1) // experts
         table = route_table(u_norm, topk_ids, w_router, w_gate.shape[0], capacity)

time: 262 us -> 244 us (0.931)
  matrix products: 29.3 us -> 19.7 us
  local copies, waits for them, and re-layouts: 12.6 us -> 8.48 us
  Pallas kernels: 210 us -> 207 us
    dot_general x2 -> x0, matrix products: 12.8 us -> none  [the longest x1 10.4 us: attention_block(): jnp.dot(heads_out.reshape(tokens, heads * VALUE_DIM), w_out, preferred_el...]
    pallas_call x0 -> x1, Pallas kernels: none -> 12 us  [out_proj(): pl.pallas_call(out_proj_kernel, grid=(heads // HEADS_STEP,), out_shape=(r...]
    pallas_call x1, Pallas kernels: 35.1 us -> 27.5 us  [attend(): pl.pallas_call(functools.partial(attend_kernel, heads), grid=(tokens // s...]
    pallas_call x1, Pallas kernels: 175 us -> 168 us  [moe_block(): pl.pallas_call(functools.partial(moe_kernel, chips, capacity), out_shape=...]
    reshape x1 -> x0, local copies, waits for them, and re-layouts: 3.94 us -> none  [attention_block(): w_uv.reshape(kv_rank, heads, VALUE_DIM)]
    dot_general x1, matrix products: 1.48 us -> 5.16 us  [attention_block(): jnp.dot(c_q, w_uq, preferred_element_type=jnp.float32).astype(jnp.bfloat16)]
    unnamed x23 -> x19, local copies, waits for them, and re-layouts: 7.52 us -> 6.51 us
where the time goes in v3:
time: 244 us
  Pallas kernels  207 us (85%)
  matrix products  19.7 us (8%)
  local copies, waits for them, and re-layouts  8.48 us (3%)
  other arithmetic  7.58 us (3%)
    pallas_call x1, Pallas kernels, moe_block(): pl.pallas_call(functools.partial(moe_kernel, chips, capacity), out_shape=...  168 us
    pallas_call x1, Pallas kernels, attend(): pl.pallas_call(functools.partial(attend_kernel, heads), grid=(tokens // s...  27.5 us
    pallas_call x1, Pallas kernels, out_proj(): pl.pallas_call(out_proj_kernel, grid=(heads // HEADS_STEP,), out_shape=(r...  12 us
    dot_general x1, matrix products, attention_block(): jnp.dot(normed, w_dq, preferred_element_type=jnp.float32)  7.85 us
    unnamed x19, local copies, waits for them, and re-layouts  6.51 us
    dot_general x1, matrix products, attention_block(): kv_proj = jnp.dot(normed, w_dkv, preferred_element_type=jnp.float32)  5.31 us
    dot_general x1, matrix products, attention_block(): jnp.dot(c_q, w_uq, preferred_element_type=jnp.float32).astype(jnp.bfloat16)  5.16 us

profile of v3, /device:TPU:112, one launch (start us, length us, event | category | flops | bytes accessed | tf_op | source)
XLA Modules:
  0.0 243.8 jit_solution(8727330075368050627)
XLA Ops:
  0.6 0.7 convert_element_type.59
  1.3 1.6 fusion
  3.0 0.7 fusion.20
  3.7 0.7 convert_element_type.61
  4.4 0.1 and_select_fusion
  4.5 0.7 convert_element_type.54
  5.2 0.7 convert_element_type.52
  5.9 0.7 broadcast_in_dim.12.gain_ref
  6.6 0.8 copy.59.position_ref
  7.4 0.0 copy-start
  7.4 5.3 %fusion.15 = f32[128,576]{1,0:T(8,128)S(1)} fusion(bf16[5120,576]{0,1:T(8,128)(2,1)} %param.31, bf16[128,5120]{1,0:T(8,128)(2,1)} %hidden_ref.1, f32[5120]{0:T(1024)S(1)} %convert_element_type.52, f32[128]{0:T(128)S(1)} %add_rsqrt_fusion.2), kind=kOutput, calls=%fused_computation.23 | convolution fusion | flops 757596160 | bytes 7524864 | tf_op jit(solution)/shard_map/dot_general | solution.py:177
  12.7 0.1 multiply_reduce_fusion.1
  12.9 0.1 multiply_convert_fusion.2.c_new_ref
  13.0 0.0 copy-start.5
  13.0 0.3 subtract_convert_fusion.1
  13.3 0.1 pad_maximum_fusion.2
  13.4 0.1 pad_maximum_fusion.1.k_new_ref
  13.5 0.7 copy.60
  14.2 0.0 copy-done
  14.2 7.9 %multiply_reduce_fusion = (f32[128]{0:T(128)S(1)}, f32[128,1536]{1,0:T(8,128)S(1)}) fusion(bf16[5120,1536]{1,0:T(8,128)(2,1)} %param.28, bf16[128,5120]{1,0:T(8,128)(2,1)S(1)} %copy-done, f32[5120]{0:T(1024)S(1)} %convert_element_type.52, f32[128]{0:T(128)S(1)} %add_rsqrt_fusion.2), kind=kOutput, calls=%fused_computation.17 | convolution fusion | flops 2016280448 | bytes 17847296 | tf_op jit(solution)/shard_map/dot_general | solution.py:173
  22.1 5.2 %convolution_convert_fusion = bf16[128,3072]{1,0:T(8,128)(2,1)S(1)} fusion(bf16[1536,3072]{1,0:T(8,128)(2,1)} %param.30, f32[128,1536]{1,0:T(8,128)S(1)} %get-tuple-element.26, f32[1536]{0:T(1024)S(1)} %convert_element_type.54, f32[128]{0:T(128)S(1)} %add_rsqrt_fusion.1), kind=kOutput, calls=%fused_computation | convolution fusion | flops 1208942592 | bytes 11016704 | tf_op jit(solution)/shard_map/dot_general | solution.py:174
  27.2 0.4 copy.51
  27.7 0.3 copy.63
  28.1 0.1 convert_element_type.58
  28.2 0.0 copy-start.6
  28.2 0.4 subtract_convert_fusion
  28.6 0.3 maximum_bitcast_fusion
  28.9 0.3 pad_maximum_fusion.q_rot_ref
  29.2 0.5 copy-done.6
  29.8 0.0 copy-start.2
  29.8 0.8 fusion.6.q_abs_ref
  30.5 0.0 copy-done.5
  30.5 1.4 copy-done.2
  32.0 0.0 copy-start.3
  32.0 27.5 %attend.1.context_ref = bf16[16,128,512]{2,1,0:T(8,128)(2,1)S(1)} custom-call(s32[128,1]{1,0:T(8,128)S(1)} %copy.59.position_ref, bf16[16,128,512]{2,1,0:T(8,128)(2,1)S(1)} %fusion.6.q_abs_ref, bf16[16,128,128]{2,1,0:T(8,128)(2,1)S(1)} %pad_maximum_fusion.q_rot_ref, bf16[128,256,512]{2,1,0:T(8,128)(2,1)} %ckv_ref.1, bf16[128,64,256]{2,1,0:T(8,128)(2,1)S(1)} %bitcast.22, ...), custom_call_target="tpu_custom_call" | custom-call | tf_op jit(solution)/shard_map/attend/pallas_call | solution.py:101
  59.5 0.0 copy-done.3
  59.5 0.0 copy-start.7
  59.5 12.0 %out_proj.1 = (bf16[128,5120]{1,0:T(8,128)(2,1)S(1)}, bf16[128,5120]{1,0:T(8,128)(2,1)S(1)}) custom-call(bf16[16,128,512]{2,1,0:T(8,128)(2,1)S(1)} %attend.1.context_ref, bf16[512,2048]{1,0:T(8,128)(2,1)S(1)} %copy-done.3, bf16[2048,5120]{1,0:T(8,128)(2,1)} %out_ref.1, bf16[128,5120]{1,0:T(8,128)(2,1)S(1)} %copy-done, ...), custom_call_target="tpu_custom_call" | custom-call | tf_op jit(solution)/shard_map/out_proj/pallas_call | solution.py:150
  71.5 0.0 copy-start.1
  71.6 0.0 copy-start.4
  71.6 1.0 copy-done.1
  72.6 0.0 copy-done.7
  72.6 0.5 select_reduce_fusion
  73.1 0.0 copy-done.4
  73.1 0.6 maximum_bitcast_fusion.1.table_ref
  73.7 167.7 %moe.1 = bf16[128,5120]{1,0:T(8,128)(2,1)} custom-call(bf16[128,5120]{1,0:T(8,128)(2,1)} %copy-done.1, bf16[128,5120]{1,0:T(8,128)(2,1)} %copy-done.4, f32[24,128]{1,0:T(8,128)} %maximum_bitcast_fusion.1.table_ref, bf16[2,5120,1536]{2,1,0:T(8,128)(2,1)} %gate_ref.1, bf16[2,5120,1536]{2,1,0:T(8,128)(2,1)} %up_ref.1, bf16[2,1536,5120]{2,1,0:T(8,128)(2,1)} %down_ref.1, ...), custom_call_target="tpu_custom_call" | custom-call | tf_op jit(solution)/shard_map/moe/pallas_call | solution.py:597
  241.4 2.5 %copy.72 = bf16[128,5120]{1,0:T(8,128)(2,1)} copy(bf16[128,5120]{1,0:T(8,128)(2,1)} %moe.1) | data formatting | bytes 2621440
  (7 shorter events, 0.1 us)
Async XLA Ops:
  7.4 6.8 %copy-start = (bf16[128,5120]{1,0:T(8,128)(2,1)S(1)}, bf16[128,5120]{1,0:T(8,128)(2,1)}, u32[]{:S(2)}) copy-start(bf16[128,5120]{1,0:T(8,128)(2,1)} %hidden_ref.1) | copy-start | bytes 3932164
  13.0 17.6 %copy-start.5 = (bf16[128,512]{1,0:T(8,128)(2,1)}, bf16[128,512]{1,0:T(8,128)(2,1)S(1)}, u32[]{:S(2)}) copy-start(bf16[128,512]{1,0:T(8,128)(2,1)S(1)} %multiply_convert_fusion.2.c_new_ref) | copy-start | bytes 393220
  28.2 1.6 copy-start.6
  29.8 2.2 copy-start.2
  32.0 27.5 %copy-start.3 = (bf16[512,2048]{1,0:T(8,128)(2,1)S(1)}, bf16[512,2048]{1,0:T(8,128)(2,1)}, u32[]{:S(2)}) copy-start(bf16[512,2048]{1,0:T(8,128)(2,1)} %uv_ref.1) | copy-start | bytes 6291460
  59.5 13.1 %copy-start.7 = (bf16[5120,16]{0,1:T(8,128)(2,1)S(1)}, bf16[5120,16]{0,1:T(8,128)(2,1)}, u32[]{:S(2)}) copy-start(bf16[5120,16]{0,1:T(8,128)(2,1)} %param.37) | copy-start | bytes 491524
  71.5 1.1 copy-start.1
  71.6 1.5 copy-start.4
